TPU v7x, 32 devices: a 4x4x1 block of a 4x4x8 slice. The times are simulated.
32 devices in a mesh: pairs: 1 (over z), ho: 4 (over y), tp: 8 (over x, core).
Axes of the slice: x: 4, y: 4, z: 1, core: 2. Of those that a mesh axis runs over, the one named last changes fastest.
The devices are a block of a 4x4x8 slice.
Arguments:
- prompt_a: bfloat16 [4, 512, 3072], P('pairs')
- prompt_b: bfloat16 [4, 512, 3072], P('pairs')
- first_a: bfloat16 [4, 3072], P(('pairs', 'ho'))
- first_b: bfloat16 [4, 3072], P(('pairs', 'ho'))
- w_qkv: bfloat16 [6, 3072, 8, 5, 128], P(None, None, 'tp')
- w_out: bfloat16 [6, 8, 3, 128, 3072], P(None, 'tp')
- w_gate: bfloat16 [6, 3072, 8192], P(None, None, 'tp')
- w_up: bfloat16 [6, 3072, 8192], P(None, None, 'tp')
- w_down: bfloat16 [6, 8192, 3072], P(None, 'tp')
- norm_attn: float32 [6, 3072], replicated
- norm_mlp: float32 [6, 3072], replicated
Outputs:
- output 1: bfloat16 [4, 512, 3072], P(('pairs', 'ho'))
- output 2: bfloat16 [4, 512, 3072], P(('pairs', 'ho'))
- output 3: float32 [4, 3072], P(('pairs', 'ho'))
- output 4: float32 [4, 3072], P(('pairs', 'ho'))
- output 5: bfloat16 [4, 6, 2, 513, 8, 128], P(('pairs', 'ho'), None, None, None, 'tp')
- output 6: bfloat16 [4, 6, 2, 513, 8, 128], P(('pairs', 'ho'), None, None, None, 'tp')
All inputs are finite; a program needn't handle non-finite values.
Results may differ from a plain program's by a relative error of at most 0.02.
Values are sent between devices in bfloat16 or wider.
A program may use at most 768 MiB of HBM per device.

v0:
```python
import jax
import jax.numpy as jnp
from jax import lax
from jax.sharding import PartitionSpec as P


def rms_norm(hidden, gain_vec):
    hidden_f = hidden.astype(jnp.float32)
    inv_rms = lax.rsqrt(jnp.mean(hidden_f * hidden_f, axis=-1, keepdims=True) + 1e-5)
    return (hidden_f * inv_rms * gain_vec).astype(jnp.bfloat16)


def causal_attention(q_heads, key_rows, value_rows):
    tokens = q_heads.shape[0]
    head_dim = q_heads.shape[-1]
    scores = jnp.einsum('tkgc,skc->kgts', q_heads, key_rows, preferred_element_type=jnp.float32) * head_dim ** -0.5
    positions = jnp.arange(tokens)
    scores = jnp.where(positions[:, None] >= positions[None, :], scores, -1e30)
    attn_probs = jax.nn.softmax(scores, axis=-1).astype(jnp.bfloat16)
    mixed_out = jnp.einsum('kgts,skc->tkgc', attn_probs, value_rows, preferred_element_type=jnp.float32)
    return mixed_out.astype(jnp.bfloat16)


def prefill_layer(hidden, layer_weights):
    w_qkv, w_out, w_gate, w_up, w_down, gain_attn, gain_mlp = layer_weights
    group_size = w_out.shape[1]
    normed = rms_norm(hidden, gain_attn)
    qkv_out = jnp.einsum('td,dkgc->tkgc', normed, w_qkv, preferred_element_type=jnp.float32).astype(jnp.bfloat16)
    key_rows = qkv_out[:, :, group_size]
    value_rows = qkv_out[:, :, group_size + 1]
    mixed_out = causal_attention(qkv_out[:, :, :group_size], key_rows, value_rows)
    attn_part = jnp.einsum('tkgc,kgcd->td', mixed_out, w_out, preferred_element_type=jnp.float32).astype(jnp.bfloat16)
    hidden = (hidden.astype(jnp.float32) + lax.psum(attn_part, 'tp').astype(jnp.float32)).astype(jnp.bfloat16)
    normed = rms_norm(hidden, gain_mlp)
    gate_pre = jnp.dot(normed, w_gate, preferred_element_type=jnp.float32)
    up_val = jnp.dot(normed, w_up, preferred_element_type=jnp.float32)
    act_out = (jax.nn.silu(gate_pre) * up_val).astype(jnp.bfloat16)
    mlp_part = jnp.dot(act_out, w_down, preferred_element_type=jnp.float32).astype(jnp.bfloat16)
    hidden = (hidden.astype(jnp.float32) + lax.psum(mlp_part, 'tp').astype(jnp.float32)).astype(jnp.bfloat16)
    return hidden, key_rows, value_rows


def decode_layer(dec_state, layer_weights, kv_layer):
    w_qkv, w_out, w_gate, w_up, w_down, gain_attn, gain_mlp = layer_weights
    group_size = w_out.shape[1]
    head_dim = w_out.shape[2]
    normed = rms_norm(dec_state, gain_attn)
    qkv_out = jnp.einsum('d,dkgc->kgc', normed, w_qkv, preferred_element_type=jnp.float32).astype(jnp.bfloat16)
    new_kv = jnp.moveaxis(qkv_out[:, group_size:], 1, 0)[:, None]
    full_kv = jnp.concatenate([kv_layer, new_kv], axis=1)
    scores = jnp.einsum('kgc,skc->kgs', qkv_out[:, :group_size], full_kv[0], preferred_element_type=jnp.float32) * head_dim ** -0.5
    attn_probs = jax.nn.softmax(scores, axis=-1).astype(jnp.bfloat16)
    mixed_out = jnp.einsum('kgs,skc->kgc', attn_probs, full_kv[1], preferred_element_type=jnp.float32).astype(jnp.bfloat16)
    attn_part = jnp.einsum('kgc,kgcd->d', mixed_out, w_out, preferred_element_type=jnp.float32)
    dec_state = dec_state + lax.psum(attn_part, 'tp')
    normed = rms_norm(dec_state, gain_mlp)
    gate_pre = jnp.dot(normed, w_gate, preferred_element_type=jnp.float32)
    up_val = jnp.dot(normed, w_up, preferred_element_type=jnp.float32)
    act_out = (jax.nn.silu(gate_pre) * up_val).astype(jnp.bfloat16)
    mlp_part = jnp.dot(act_out, w_down, preferred_element_type=jnp.float32)
    dec_state = dec_state + lax.psum(mlp_part, 'tp')
    return dec_state, full_kv


def decode_all(first_tok, received, layer_list):
    dec_state = first_tok.astype(jnp.float32)
    caches = []
    for layer_idx, layer_weights in enumerate(layer_list):
        dec_state, full_kv = decode_layer(dec_state, layer_weights, received[layer_idx])
        caches.append(full_kv)
    return dec_state, jnp.stack(caches)


def device_specs():
    row_axes = ('pairs', 'ho')
    in_specs = (P('pairs', None, None), P('pairs', None, None), P(row_axes, None), P(row_axes, None),
                P(None, None, 'tp', None, None), P(None, 'tp', None, None, None), P(None, None, 'tp'),
                P(None, None, 'tp'), P(None, 'tp', None), P(None, None), P(None, None))
    out_specs = (P(row_axes, None, None), P(row_axes, None, None), P(row_axes, None), P(row_axes, None),
                 P(row_axes, None, None, None, 'tp', None), P(row_axes, None, None, None, 'tp', None))
    return in_specs, out_specs


def solution(mesh):
    ho_size = mesh.shape['ho']
    hand_pairs = [(source_idx, (source_idx + 1) % ho_size) for source_idx in range(ho_size)]
    in_specs, out_specs = device_specs()

    def per_device(prompt_a, prompt_b, first_a, first_b, w_qkv, w_out, w_gate, w_up, w_down, norm_attn, norm_mlp):
        weights = (w_qkv, w_out, w_gate, w_up, w_down, norm_attn, norm_mlp)
        layer_list = [tuple(stacked[layer_idx] for stacked in weights) for layer_idx in range(w_qkv.shape[0])]
        ho_index = lax.axis_index('ho')
        hidden_a = lax.dynamic_index_in_dim(prompt_a, ho_index, 0, keepdims=False)
        hidden_b = lax.dynamic_index_in_dim(prompt_b, ho_index, 0, keepdims=False)
        kv_a = []
        kv_b = []
        for layer_weights in layer_list:
            hidden_a, key_rows, value_rows = prefill_layer(hidden_a, layer_weights)
            kv_a.append(jnp.stack([key_rows, value_rows]))
            hidden_b, key_rows, value_rows = prefill_layer(hidden_b, layer_weights)
            kv_b.append(jnp.stack([key_rows, value_rows]))
        recv_a = lax.ppermute(jnp.stack(kv_a), 'ho', hand_pairs)
        recv_b = lax.ppermute(jnp.stack(kv_b), 'ho', hand_pairs)
        final_a, cache_a = decode_all(first_a[0], recv_a, layer_list)
        final_b, cache_b = decode_all(first_b[0], recv_b, layer_list)
        return hidden_a[None], hidden_b[None], final_a[None], final_b[None], cache_a[None], cache_b[None]

    return jax.shard_map(per_device, mesh=mesh, in_specs=in_specs, out_specs=out_specs, check_vma=False)
```

profile of v0, /device:TPU:97, one launch (start us, length us, event | category | flops | bytes accessed | tf_op | source)
XLA Modules:
  0.0 2398.8 jit_solution(1477347358587200134)
XLA Ops:
  26.5 64.4 %all-reduce.57.cloned.1.call-done = bf16[512,3072]{1,0:T(8,128)(2,1)} async-done(((bf16[512,3072]{1,0:T(8,128)(2,1)}), bf16[512,3072]{1,0:T(8,128)(2,1)}) %all-reduce.57.cloned.1.call-update) | async-done | bytes 3145744 | tf_op jit(solution)/shard_map/psum | solution.py:33
  116.8 63.4 %all-reduce.59.cloned.1.call-done = bf16[512,3072]{1,0:T(8,128)(2,1)} async-done(((bf16[512,3072]{1,0:T(8,128)(2,1)}), bf16[512,3072]{1,0:T(8,128)(2,1)}) %all-reduce.59.cloned.1.call-update) | async-done | bytes 3145744 | tf_op jit(solution)/shard_map/psum | solution.py:39
  199.9 63.3 %all-reduce.61.cloned.1.call-done = bf16[512,3072]{1,0:T(8,128)(2,1)} async-done(((bf16[512,3072]{1,0:T(8,128)(2,1)}), bf16[512,3072]{1,0:T(8,128)(2,1)}) %all-reduce.61.cloned.1.call-update) | async-done | bytes 3145744 | tf_op jit(solution)/shard_map/psum | solution.py:33
  289.9 63.1 %all-reduce.63.cloned.1.call-done = bf16[512,3072]{1,0:T(8,128)(2,1)} async-done(((bf16[512,3072]{1,0:T(8,128)(2,1)}), bf16[512,3072]{1,0:T(8,128)(2,1)}) %all-reduce.63.cloned.1.call-update) | async-done | bytes 3145744 | tf_op jit(solution)/shard_map/psum | solution.py:39
  372.7 63.4 %all-reduce.65.cloned.1.call-done = bf16[512,3072]{1,0:T(8,128)(2,1)} async-done(((bf16[512,3072]{1,0:T(8,128)(2,1)}), bf16[512,3072]{1,0:T(8,128)(2,1)}) %all-reduce.65.cloned.1.call-update) | async-done | bytes 3145744 | tf_op jit(solution)/shard_map/psum | solution.py:33
  462.5 63.4 %all-reduce.67.cloned.1.call-done = bf16[512,3072]{1,0:T(8,128)(2,1)} async-done(((bf16[512,3072]{1,0:T(8,128)(2,1)}), bf16[512,3072]{1,0:T(8,128)(2,1)}) %all-reduce.67.cloned.1.call-update) | async-done | bytes 3145744 | tf_op jit(solution)/shard_map/psum | solution.py:39
  543.1 63.3 %all-reduce.69.cloned.1.call-done = bf16[512,3072]{1,0:T(8,128)(2,1)} async-done(((bf16[512,3072]{1,0:T(8,128)(2,1)}), bf16[512,3072]{1,0:T(8,128)(2,1)}) %all-reduce.69.cloned.1.call-update) | async-done | bytes 3145744 | tf_op jit(solution)/shard_map/psum | solution.py:33
  644.2 54.0 %all-reduce.71.cloned.1.call-done = bf16[512,3072]{1,0:T(8,128)(2,1)} async-done(((bf16[512,3072]{1,0:T(8,128)(2,1)}), bf16[512,3072]{1,0:T(8,128)(2,1)}) %all-reduce.71.cloned.1.call-update) | async-done | bytes 3145744 | tf_op jit(solution)/shard_map/psum | solution.py:39
  717.4 63.4 %all-reduce.73.cloned.1.call-done = bf16[512,3072]{1,0:T(8,128)(2,1)} async-done(((bf16[512,3072]{1,0:T(8,128)(2,1)}), bf16[512,3072]{1,0:T(8,128)(2,1)}) %all-reduce.73.cloned.1.call-update) | async-done | bytes 3145744 | tf_op jit(solution)/shard_map/psum | solution.py:33
  809.2 63.4 %all-reduce.75.cloned.1.call-done = bf16[512,3072]{1,0:T(8,128)(2,1)} async-done(((bf16[512,3072]{1,0:T(8,128)(2,1)}), bf16[512,3072]{1,0:T(8,128)(2,1)}) %all-reduce.75.cloned.1.call-update) | async-done | bytes 3145744 | tf_op jit(solution)/shard_map/psum | solution.py:39
  890.7 63.3 %all-reduce.37.cloned.1.call-done = bf16[512,3072]{1,0:T(8,128)(2,1)} async-done(((bf16[512,3072]{1,0:T(8,128)(2,1)}), bf16[512,3072]{1,0:T(8,128)(2,1)}) %all-reduce.37.cloned.1.call-update) | async-done | bytes 3145744 | tf_op jit(solution)/shard_map/psum | solution.py:33
  980.2 63.1 %all-reduce.39.cloned.1.call-done = bf16[512,3072]{1,0:T(8,128)(2,1)} async-done(((bf16[512,3072]{1,0:T(8,128)(2,1)}), bf16[512,3072]{1,0:T(8,128)(2,1)}) %all-reduce.39.cloned.1.call-update) | async-done | bytes 3145744 | tf_op jit(solution)/shard_map/psum | solution.py:39
  1063.5 63.4 %all-reduce.41.cloned.1.call-done = bf16[512,3072]{1,0:T(8,128)(2,1)} async-done(((bf16[512,3072]{1,0:T(8,128)(2,1)}), bf16[512,3072]{1,0:T(8,128)(2,1)}) %all-reduce.41.cloned.1.call-update) | async-done | bytes 3145744 | tf_op jit(solution)/shard_map/psum | solution.py:33
  1153.3 63.4 %all-reduce.43.cloned.1.call-done = bf16[512,3072]{1,0:T(8,128)(2,1)} async-done(((bf16[512,3072]{1,0:T(8,128)(2,1)}), bf16[512,3072]{1,0:T(8,128)(2,1)}) %all-reduce.43.cloned.1.call-update) | async-done | bytes 3145744 | tf_op jit(solution)/shard_map/psum | solution.py:39
  1233.8 63.3 %all-reduce.45.cloned.1.call-done = bf16[512,3072]{1,0:T(8,128)(2,1)} async-done(((bf16[512,3072]{1,0:T(8,128)(2,1)}), bf16[512,3072]{1,0:T(8,128)(2,1)}) %all-reduce.45.cloned.1.call-update) | async-done | bytes 3145744 | tf_op jit(solution)/shard_map/psum | solution.py:33
  1325.7 63.1 %all-reduce.47.cloned.1.call-done = bf16[512,3072]{1,0:T(8,128)(2,1)} async-done(((bf16[512,3072]{1,0:T(8,128)(2,1)}), bf16[512,3072]{1,0:T(8,128)(2,1)}) %all-reduce.47.cloned.1.call-update) | async-done | bytes 3145744 | tf_op jit(solution)/shard_map/psum | solution.py:39
  1414.6 54.7 %all-reduce.49.cloned.1.call-done = bf16[512,3072]{1,0:T(8,128)(2,1)} async-done(((bf16[512,3072]{1,0:T(8,128)(2,1)}), bf16[512,3072]{1,0:T(8,128)(2,1)}) %all-reduce.49.cloned.1.call-update) | async-done | bytes 3145744 | tf_op jit(solution)/shard_map/psum | solution.py:33
  1507.4 53.6 %all-reduce.51.cloned.1.call-done = bf16[512,3072]{1,0:T(8,128)(2,1)} async-done(((bf16[512,3072]{1,0:T(8,128)(2,1)}), bf16[512,3072]{1,0:T(8,128)(2,1)}) %all-reduce.51.cloned.1.call-update) | async-done | bytes 3145744 | tf_op jit(solution)/shard_map/psum | solution.py:39
  1587.5 55.3 %all-reduce.53.cloned.1.call-done = bf16[512,3072]{1,0:T(8,128)(2,1)} async-done(((bf16[512,3072]{1,0:T(8,128)(2,1)}), bf16[512,3072]{1,0:T(8,128)(2,1)}) %all-reduce.53.cloned.1.call-update) | async-done | bytes 3145744 | tf_op jit(solution)/shard_map/psum | solution.py:33
  1681.7 52.8 %all-reduce.55.cloned.1.call-done = bf16[512,3072]{1,0:T(8,128)(2,1)} async-done(((bf16[512,3072]{1,0:T(8,128)(2,1)}), bf16[512,3072]{1,0:T(8,128)(2,1)}) %all-reduce.55.cloned.1.call-update) | async-done | bytes 3145744 | tf_op jit(solution)/shard_map/psum | solution.py:39
  1782.6 26.5 %all-reduce.11 = (f32[3072]{0:T(1024)S(1)}, f32[3072]{0:T(1024)S(1)}) all-reduce(f32[3072]{0:T(1024)S(1)} %bitcast.1822, f32[3072]{0:T(1024)S(1)} %bitcast.1810), channel_id=1, replica_groups=mesh['pairs'=1,'ho'=4,'tp'=8] {'tp'}, use_global_device_ids=true, to_apply=%region_75.76 | all-reduce | flops 6144 | bytes 49152 | tf_op jit(solution)/shard_map/psum | solution.py:55
  1833.5 23.9 all-reduce.10
  1871.1 24.1 %all-reduce.9 = (f32[3072]{0:T(1024)S(1)}, f32[3072]{0:T(1024)S(1)}) all-reduce(f32[3072]{0:T(1024)S(1)} %bitcast.1824, f32[3072]{0:T(1024)S(1)} %bitcast.1811), channel_id=1, replica_groups=mesh['pairs'=1,'ho'=4,'tp'=8] {'tp'}, use_global_device_ids=true, to_apply=%region_81.82 | all-reduce | flops 6144 | bytes 49152 | tf_op jit(solution)/shard_map/psum | solution.py:55
  1920.1 23.8 all-reduce.8
  1957.7 23.9 all-reduce.7
  2006.5 23.8 all-reduce.6
  2044.1 23.9 all-reduce.5
  2092.9 23.8 all-reduce.4
  2130.4 24.1 %all-reduce.3 = (f32[3072]{0:T(1024)S(1)}, f32[3072]{0:T(1024)S(1)}) all-reduce(f32[3072]{0:T(1024)S(1)} %bitcast.1830, f32[3072]{0:T(1024)S(1)} %bitcast.1814), channel_id=1, replica_groups=mesh['pairs'=1,'ho'=4,'tp'=8] {'tp'}, use_global_device_ids=true, to_apply=%region_99.100 | all-reduce | flops 6144 | bytes 49152 | tf_op jit(solution)/shard_map/psum | solution.py:55
  2179.8 23.8 all-reduce.2
  2322.6 23.9 all-reduce
  2355.1 28.9 %all-reduce.77.cloned.1.call-done = (bf16[512,3072]{1,0:T(8,128)(2,1)}, bf16[512,3072]{1,0:T(8,128)(2,1)}) async-done(((bf16[512,3072]{1,0:T(8,128)(2,1)}, bf16[512,3072]{1,0:T(8,128)(2,1)}), (bf16[512,3072]{1,0:T(8,128)(2,1)}, bf16[512,3072]{1,0:T(8,128)(2,1)})) %all-reduce.77.cloned.1.call-update) | async-done | bytes 6291472 | tf_op jit(solution)/shard_map/psum | solution.py:39
  (625 shorter events, 849.9 us)
Async XLA Ops:
  7.2 83.7 %all-reduce.57.cloned.1.call-start = ((), (), s32[]{:S(2)}) async-start(), calls=%async_computation.10 | async-start | bytes 6291456 | tf_op jit(solution)/shard_map/psum | solution.py:33
  10.6 345.6 %copy-start.74 = (f32[1,3072]{1,0:T(1,128)}, f32[1,3072]{1,0:T(1,128)S(1)}, u32[]{:S(2)}) copy-start(f32[1,3072]{1,0:T(1,128)S(1)} %get-tuple-element.164) | copy-start | bytes 36868
  10.6 518.4 %copy-start.68 = (f32[1,3072]{1,0:T(1,128)}, f32[1,3072]{1,0:T(1,128)S(1)}, u32[]{:S(2)}) copy-start(f32[1,3072]{1,0:T(1,128)S(1)} %get-tuple-element.163) | copy-start | bytes 36868
  25.0 155.2 %all-reduce.59.cloned.1.call-start = ((), (), s32[]{:S(2)}) async-start(), calls=%async_computation.11 | async-start | bytes 6291456 | tf_op jit(solution)/shard_map/psum | solution.py:39
  26.5 248.8 %copy-start.77 = (f32[1,3072]{1,0:T(1,128)}, f32[1,3072]{1,0:T(1,128)S(1)}, u32[]{:S(2)}) copy-start(f32[1,3072]{1,0:T(1,128)S(1)} %get-tuple-element.159) | copy-start | bytes 36868
  26.5 421.7 %copy-start.71 = (f32[1,3072]{1,0:T(1,128)}, f32[1,3072]{1,0:T(1,128)S(1)}, u32[]{:S(2)}) copy-start(f32[1,3072]{1,0:T(1,128)S(1)} %get-tuple-element.158) | copy-start | bytes 36868
  26.5 594.3 %copy-start.65 = (f32[1,3072]{1,0:T(1,128)}, f32[1,3072]{1,0:T(1,128)S(1)}, u32[]{:S(2)}) copy-start(f32[1,3072]{1,0:T(1,128)S(1)} %get-tuple-element.157) | copy-start | bytes 36868
  116.5 146.8 %all-reduce.61.cloned.1.call-start = ((), (), s32[]{:S(2)}) async-start(), calls=%async_computation.12 | async-start | bytes 6291456 | tf_op jit(solution)/shard_map/psum | solution.py:33
  199.6 153.4 %all-reduce.63.cloned.1.call-start = ((), (), s32[]{:S(2)}) async-start(), calls=%async_computation.13 | async-start | bytes 6291456 | tf_op jit(solution)/shard_map/psum | solution.py:39
  289.4 146.8 %all-reduce.65.cloned.1.call-start = ((), (), s32[]{:S(2)}) async-start(), calls=%async_computation.14 | async-start | bytes 6291456 | tf_op jit(solution)/shard_map/psum | solution.py:33
  372.5 153.4 %all-reduce.67.cloned.1.call-start = ((), (), s32[]{:S(2)}) async-start(), calls=%async_computation.15 | async-start | bytes 6291456 | tf_op jit(solution)/shard_map/psum | solution.py:39
  462.3 144.2 %all-reduce.69.cloned.1.call-start = ((), (), s32[]{:S(2)}) async-start(), calls=%async_computation.16 | async-start | bytes 6291456 | tf_op jit(solution)/shard_map/psum | solution.py:33
  542.8 155.5 %all-reduce.71.cloned.1.call-start = ((), (), s32[]{:S(2)}) async-start(), calls=%async_computation.17 | async-start | bytes 6291456 | tf_op jit(solution)/shard_map/psum | solution.py:39
  634.5 146.2 %all-reduce.73.cloned.1.call-start = ((), (), s32[]{:S(2)}) async-start(), calls=%async_computation.18 | async-start | bytes 6291456 | tf_op jit(solution)/shard_map/psum | solution.py:33
  717.1 155.4 %all-reduce.75.cloned.1.call-start = ((), (), s32[]{:S(2)}) async-start(), calls=%async_computation.19 | async-start | bytes 6291456 | tf_op jit(solution)/shard_map/psum | solution.py:39
  808.9 145.1 %all-reduce.37.cloned.1.call-start = ((), (), s32[]{:S(2)}) async-start(), calls=%async_computation | async-start | bytes 6291456 | tf_op jit(solution)/shard_map/psum | solution.py:33
  890.3 152.9 %all-reduce.39.cloned.1.call-start = ((), (), s32[]{:S(2)}) async-start(), calls=%async_computation.1 | async-start | bytes 6291456 | tf_op jit(solution)/shard_map/psum | solution.py:39
  979.6 147.3 %all-reduce.41.cloned.1.call-start = ((), (), s32[]{:S(2)}) async-start(), calls=%async_computation.2 | async-start | bytes 6291456 | tf_op jit(solution)/shard_map/psum | solution.py:33
  1063.3 153.4 %all-reduce.43.cloned.1.call-start = ((), (), s32[]{:S(2)}) async-start(), calls=%async_computation.3 | async-start | bytes 6291456 | tf_op jit(solution)/shard_map/psum | solution.py:39
  1153.0 144.1 %all-reduce.45.cloned.1.call-start = ((), (), s32[]{:S(2)}) async-start(), calls=%async_computation.4 | async-start | bytes 6291456 | tf_op jit(solution)/shard_map/psum | solution.py:33
  1233.5 155.3 %all-reduce.47.cloned.1.call-start = ((), (), s32[]{:S(2)}) async-start(), calls=%async_computation.5 | async-start | bytes 6291456 | tf_op jit(solution)/shard_map/psum | solution.py:39
  1325.2 144.1 %all-reduce.49.cloned.1.call-start = ((), (), s32[]{:S(2)}) async-start(), calls=%async_computation.6 | async-start | bytes 6291456 | tf_op jit(solution)/shard_map/psum | solution.py:33
  1405.7 155.3 %all-reduce.51.cloned.1.call-start = ((), (), s32[]{:S(2)}) async-start(), calls=%async_computation.7 | async-start | bytes 6291456 | tf_op jit(solution)/shard_map/psum | solution.py:39
  1497.3 145.5 %all-reduce.53.cloned.1.call-start = ((), (), s32[]{:S(2)}) async-start(), calls=%async_computation.8 | async-start | bytes 6291456 | tf_op jit(solution)/shard_map/psum | solution.py:33
  1505.9 78.1 %collective-permute-start.1 = (bf16[6,2,512,1,128]{4,2,1,3,0:T(8,128)(2,1)}, bf16[6,2,512,1,128]{4,2,1,3,0:T(8,128)(2,1)}, u32[]{:S(2)}, u32[]{:S(2)}) collective-permute-start(bf16[6,2,512,1,128]{4,2,1,3,0:T(8,128)(2,1)} %fusion.967), channel_id=1, source_target_pairs={{0,8},{8,16},{16,24},{24,0},{1,9},{9,17},{17,25},{25,1},{2,10},{10... | collective-permute-start | bytes 4718600 | tf_op jit(solution)/shard_map/ppermute | solution.py:103
  1579.1 155.4 %all-reduce.55.cloned.1.call-start = ((), (), s32[]{:S(2)}) async-start(), calls=%async_computation.9 | async-start | bytes 6291456 | tf_op jit(solution)/shard_map/psum | solution.py:39
  1670.8 579.1 %all-reduce.79.cloned.1.call-start = ((), (), s32[]{:S(2)}) async-start(), calls=%async_computation.21 | async-start | bytes 12582912 | tf_op jit(solution)/shard_map/psum | solution.py:33
  1743.7 34.6 %collective-permute-start = (bf16[6,2,512,1,128]{4,2,1,3,0:T(8,128)(2,1)}, bf16[6,2,512,1,128]{4,2,1,3,0:T(8,128)(2,1)}, u32[]{:S(2)}, u32[]{:S(2)}) collective-permute-start(bf16[6,2,512,1,128]{4,2,1,3,0:T(8,128)(2,1)} %fusion.961), channel_id=1, source_target_pairs={{0,8},{8,16},{16,24},{24,0},{1,9},{9,17},{17,25},{25,1},{2,10},{10... | collective-permute-start | bytes 4718600 | tf_op jit(solution)/shard_map/ppermute | solution.py:102
  1761.0 623.1 %all-reduce.77.cloned.1.call-start = ((), (), s32[]{:S(2)}) async-start(), calls=%async_computation.20 | async-start | bytes 12582912 | tf_op jit(solution)/shard_map/psum | solution.py:39
  1779.8 175.6 %copy-start.32 = (bf16[2,512,1,128]{3,1,0,2:T(8,128)(2,1)}, bf16[2,512,1,128]{3,1,0,2:T(8,128)(2,1)S(1)}, u32[]{:S(2)}) copy-start(bf16[2,512,1,128]{3,1,0,2:T(8,128)(2,1)S(1)} %get-tuple-element.129) | copy-start | bytes 786436
  1779.8 261.9 %copy-start.31 = (bf16[2,512,1,128]{3,1,0,2:T(8,128)(2,1)}, bf16[2,512,1,128]{3,1,0,2:T(8,128)(2,1)S(1)}, u32[]{:S(2)}) copy-start(bf16[2,512,1,128]{3,1,0,2:T(8,128)(2,1)S(1)} %get-tuple-element.128) | copy-start | bytes 786436
  1779.8 348.3 %copy-start.30 = (bf16[2,512,1,128]{3,1,0,2:T(8,128)(2,1)}, bf16[2,512,1,128]{3,1,0,2:T(8,128)(2,1)S(1)}, u32[]{:S(2)}) copy-start(bf16[2,512,1,128]{3,1,0,2:T(8,128)(2,1)S(1)} %get-tuple-element.127) | copy-start | bytes 786436
  (91 other events, 2612.7 us)
Sparse Core Ops, SparseCore 0:
  25.1 65.7 all-reduce.56
  116.6 63.5 all-reduce.58
  199.7 63.5 all-reduce.60
  289.5 63.5 all-reduce.62
  372.6 63.4 all-reduce.64
  462.4 63.4 all-reduce.66
  542.9 63.5 all-reduce.68
  634.7 63.5 all-reduce.70
  717.2 63.4 all-reduce.72
  809.0 63.4 all-reduce.74
  890.4 63.4 all-reduce.36
  979.8 63.4 all-reduce.38
  1063.4 63.4 all-reduce.40
  1153.1 63.4 all-reduce.42
  1233.6 63.5 all-reduce.44
  1325.3 63.4 all-reduce.46
  1405.8 63.4 all-reduce.48
  1497.4 63.4 all-reduce.50
  1579.2 63.5 all-reduce.52
  1671.0 63.4 all-reduce.54
  1761.0 80.3 all-reduce.78
  2304.1 79.8 all-reduce.76
where the time goes:
time: 2410 us; the launch traced here: 2400 us
  waiting for transfers between devices  1270 us (53%)
  matrix products  611 us (25%)
  blocking collectives  289 us (12%)
  other arithmetic  144 us (6%)
  local copies, waits for them, and re-layouts  43.5 us (2%)
  between operations  33.3 us (1%)
    psum x11, waiting for transfers between devices, prefill_layer(): lax.psum(mlp_part, 'tp').astype(jnp.float32)  632 us
    psum x11, waiting for transfers between devices, prefill_layer(): lax.psum(attn_part, 'tp').astype(jnp.float32)  618 us
    dot_general x12, matrix products, prefill_layer(): jnp.dot(act_out, w_down, preferred_element_type=jnp.float32)  166 us
    psum x6, blocking collectives, decode_layer(): dec_state = dec_state + lax.psum(attn_part, 'tp')  146 us
    psum x6, blocking collectives, decode_layer(): dec_state = dec_state + lax.psum(mlp_part, 'tp')  143 us
    reduce_sum x46, other arithmetic, rms_norm(): jnp.mean(hidden_f * hidden_f, axis=-1, keepdims=True) + 1e-05  110 us
    dot_general x12, matrix products, prefill_layer(): gate_pre = jnp.dot(normed, w_gate, preferred_element_type=jnp.float32)  89.9 us
    dot_general x12, matrix products, prefill_layer(): jnp.einsum('tkgc,kgcd->td', mixed_out, w_out, preferred_element_type=jnp....  78.6 us
  transfers between devices with their start and end apart: 24, of which 22 were waited for; matrix products, arithmetic and copies ran while one was open for 12% of the time, Pallas kernels for 0%

commit v1 on v0

v1 whole, which is shorter than its diff:
```python
import functools

import jax
import jax.numpy as jnp
from jax import lax
from jax.experimental import pallas as pl
from jax.experimental.pallas import tpu as pltpu
from jax.sharding import PartitionSpec as P

MESH = pl.DeviceIdType.MESH
F32 = jnp.float32
BF16 = jnp.bfloat16
CORES = 2
CHIPS = 4
STREAMS = 4
DEC = 16
PAD = 128


def tile_of(size, most):
    tile = most
    while size % tile:
        tile //= 2
    return tile


def body(cfg, pa, pb, y0, wq, wo, wg, wu, wd, g1, g2, oa, ob, fin, ca, cb,
         H, PB, PR, AR, BC, XR, QS, KV, OS, US, KVR, WQ, WO, WG, WU, WD, DY, DP, DS, DR, DG,
         s_prs, s_prr, s_as, s_ar, s_bs, s_br, s_cs, s_cr, s_gs, s_gr, s_rs, s_rr, s_ds, s_dr,
         s_kvs, s_kvr, s_wa, s_wm, s_in, s_out, s_ko, s_e1s, s_e1r, s_e2s, s_e2r, s_fin):
    n_ho, n_tp, L, T, D, G, hd, F = cfg
    TS = T // 2
    NB = n_tp
    BR = TS // NB
    DH = D // 2
    NS = 8 * L
    SL = D // n_tp
    NQ = SL // hd
    scale = hd ** -0.5
    j = lax.axis_index('ho')
    tp = lax.axis_index('tp')
    X = lax.div(tp, CORES)
    c = lax.rem(tp, CORES)
    R = lax.rem(X + 1, CHIPS)
    O = lax.rem(X + 2, CHIPS)
    Lf = lax.rem(X + 3, CHIPS)
    to_right = {'tp': R * CORES + c}
    to_left = {'tp': Lf * CORES + c}
    to_partner = {'tp': X * CORES + (1 - c)}
    ho_right = lax.rem(j + 1, n_ho)
    ho_left = lax.rem(j + n_ho - 1, n_ho)

    def rc(src, dst, ss, rs, dev):
        return pltpu.make_async_remote_copy(src_ref=src, dst_ref=dst, send_sem=ss, recv_sem=rs,
                                            device_id=dev, device_id_type=MESH)

    def lc(src, dst, sem):
        return pltpu.make_async_copy(src, dst, sem)

    def own_rows(Y):
        return pl.ds(pl.multiple_of((Y * CORES + c) * BR, BR), BR)

    def d_pr(par, h):
        return rc(PB.at[par, h, :, 1 - c], PR.at[par, h], s_prs.at[par, h], s_prr.at[par, h], to_partner)

    def d_a(par, d):
        return rc(PB.at[par, d, O, c], AR.at[par, d], s_as.at[par, d], s_ar.at[par, d], to_left if d else to_right)

    def d_b(par, d):
        return rc(PB.at[par, 1 - d, Lf if d else R, c], BC.at[par, d, 1 - d], s_bs.at[par, d], s_br.at[par, d],
                  to_left if d else to_right)

    def d_c(par, d):
        return rc(PB.at[par, d, Lf if d else R, c], BC.at[par, d, d], s_cs.at[par, d], s_cr.at[par, d],
                  to_left if d else to_right)

    def h_part(s, Y, half):
        return H.at[s, own_rows(Y), pl.ds(half * DH, DH)]

    def d_g(s, par, d, half):
        return rc(h_part(s, X, half), h_part(s, X, half), s_gs.at[par, d, half], s_gr.at[par, d, half],
                  to_left if d else to_right)

    def d_r(s, par, d):
        Y = R if d else Lf
        return rc(h_part(s, Y, d), h_part(s, Y, d), s_rs.at[par, d], s_rr.at[par, d], to_left if d else to_right)

    def d_d(s, Y):
        return rc(H.at[s, own_rows(Y)], H.at[s, own_rows(Y)], s_ds.at[s], s_dr.at[s], to_partner)

    def d_d_all(s):
        return rc(H.at[s, pl.ds(0, CHIPS * BR)], H.at[s, pl.ds(0, CHIPS * BR)], s_ds.at[s], s_dr.at[s], to_partner)

    def d_kv(l, pr):
        return rc(KV.at[pr], KVR.at[l, pr, :, pl.ds(0, T)], s_kvs.at[pr], s_kvr.at[l, pr], {'ho': ho_right})

    def wa_copies(l):
        out = [lc(wq.at[l, i], WQ.at[:, pl.ds(i * hd, hd)], s_wa.at[i]) for i in range(G + 2)]
        return out + [lc(wo.at[l], WO, s_wa.at[G + 2])]

    def wm_copies(l):
        return [lc(wg.at[l], WG, s_wm.at[0]), lc(wu.at[l], WU, s_wm.at[1]), lc(wd.at[l], WD, s_wm.at[2])]

    def prompt_copy(s):
        src = pa if s < 2 else pb
        return lc(src.at[j, pl.ds((s % 2) * TS, TS)], H.at[s, pl.ds(0, TS)], s_in.at[s])

    barrier = pltpu.get_barrier_semaphore()
    for k in range(1, n_tp):
        pl.semaphore_signal(barrier, inc=1, device_id={'tp': lax.rem(tp + k, n_tp)}, device_id_type=MESH)
    for k in (ho_right, ho_left):
        pl.semaphore_signal(barrier, inc=1, device_id={'ho': k}, device_id_type=MESH)

    prompt_copy(0).start()
    for w in wa_copies(0):
        w.start()
    for s in range(1, STREAMS):
        prompt_copy(s).start()
    for w in wm_copies(0):
        w.start()
    KV[...] = jnp.zeros(KV.shape, BF16)
    for s in range(STREAMS):
        H[s, TS:TS + DEC, :] = jnp.zeros((DEC, D), BF16)

    def zero_kvr(l, _):
        for pr in range(2):
            for kv in range(2):
                KVR[l, pr, kv, T:T + PAD, :] = jnp.zeros((PAD, hd), BF16)
        return 0

    lax.fori_loop(0, L, zero_kvr, 0)

    def normed(xf, gain):
        ms = jnp.mean(xf * xf, axis=-1, keepdims=True)
        return xf * lax.rsqrt(ms + 1e-5) * gain

    def decode_norm(gain):
        h = normed(DY[...], gain)
        H[STREAMS - 1, TS:TS + DEC, :] = jnp.concatenate([h, jnp.zeros_like(h)], axis=0).astype(BF16)

    DY[...] = y0[...]
    decode_norm(g1[0:1, :])
    pl.semaphore_wait(barrier, n_tp - 1 + 2)

    def slot(it, _):
        n = it - 1
        m1, m2, m3, mc = n - 1, n - 2, n - 3, n + 1
        live_n = jnp.logical_and(n >= 0, n < NS)
        live_1 = jnp.logical_and(m1 >= 0, m1 < NS)
        live_2 = jnp.logical_and(m2 >= 0, m2 < NS)
        live_3 = jnp.logical_and(m3 >= 0, m3 < NS)
        live_c = mc < NS
        par_n = lax.rem(n + 8, 2)
        par_1 = lax.rem(m1 + 8, 2)

        @pl.when(live_n)
        def _():
            par = par_n
            for h in range(2):
                d_pr(par, h).wait_recv()

            def add(h, Y):
                PB[par, h, Y, c] = PB[par, h, Y, c] + PR[par, h, Y]

            add(0, O)
            add(1, O)
            add(1, R)
            add(0, Lf)
            for d in range(2):
                d_a(par, d).start()
            for d in range(2):
                d_b(par, d).start()
            add(0, R)
            add(1, Lf)
            add(0, X)
            add(1, X)

        @pl.when(live_1)
        def _():
            par = par_1
            s = lax.rem(m1, STREAMS)
            l = lax.div(m1, 8)
            is_attn = lax.rem(lax.div(m1, 4), 2) == 0
            last = m1 >= NS - STREAMS
            for d in range(2):
                d_b(par, d).wait_recv()
            for d in range(2):
                d_c(par, d).wait_recv()
            x_new = []
            ms = jnp.zeros((BR, 1), F32)
            for h in range(2):
                total = PB[par, h, X, c].astype(F32) + (BC[par, 0, h].astype(F32) + BC[par, 1, h].astype(F32))
                x = XR[s, :, h * DH:(h + 1) * DH].astype(F32) + total.astype(BF16).astype(F32)
                x = x.astype(BF16)
                XR[s, :, h * DH:(h + 1) * DH] = x
                x = x.astype(F32)
                ms = ms + jnp.sum(x * x, axis=-1, keepdims=True)
                x_new.append(x)
            inv = lax.rsqrt(ms * (1.0 / D) + 1e-5)
            nl = jnp.minimum(l + 1, L - 1)
            for h in range(2):
                cols = slice(h * DH, (h + 1) * DH)
                gain = jnp.where(is_attn, g2[pl.ds(l, 1), cols], g1[pl.ds(nl, 1), cols])
                hn = x_new[h] * inv * gain
                H[s, own_rows(X), cols] = jnp.where(last, x_new[h], hn).astype(BF16)
            for half in range(2):
                for d in range(2):
                    d_g(s, par, d, half if d == 0 else 1 - half).start()
            d_d(s, X).start()

        @pl.when(live_1)
        def _():
            for h in range(2):
                d_pr(par_1, h).wait_send()
            for d in range(2):
                d_a(par_1, d).wait_send()
                d_b(par_1, d).wait_send()
                d_c(par_1, d).wait_send()

        @pl.when(live_2)
        def _():
            par = lax.rem(m2, 2)
            s = lax.rem(m2, STREAMS)
            d_g(s, par, 0, 1).wait_recv()
            d_d(s, Lf).start()
            d_g(s, par, 1, 0).wait_recv()
            d_d(s, R).start()
            for d in range(2):
                d_r(s, par, d).wait_recv()
            d_d(s, O).start()
            for d in range(2):
                for half in range(2):
                    d_g(s, par, d, half).wait_send()
                d_r(s, par, d).wait_send()

        @pl.when(live_3)
        def _():
            s = lax.rem(m3, STREAMS)
            d_d_all(s).wait_recv()
            d_d_all(s).wait_send()

        for s in range(STREAMS):
            @pl.when(m3 == NS - STREAMS + s)
            def _():
                lc(H.at[s, pl.ds(0, TS)], (oa if s < 2 else ob).at[pl.ds((s % 2) * TS, TS)], s_out.at[s]).start()

        r8 = lax.rem(mc, 8)

        @pl.when(jnp.logical_or(r8 == 5, jnp.logical_and(r8 == 0, mc > 0)))
        def _():
            rc(DS.at[pl.ds(0, n_tp - 1)], DR.at[pl.ds(0, n_tp - 1)], s_e1s, s_e1r, to_partner).wait_recv()
            rc(DS.at[pl.ds(0, n_tp - 1)], DR.at[pl.ds(0, n_tp - 1)], s_e1s, s_e1r, to_partner).wait_send()
            acc = DR[0]
            for k in range(1, n_tp):
                acc = acc + DR[k]
            DG[tp] = acc
            for k in range(1, n_tp):
                rc(DG.at[tp], DG.at[tp], s_e2s, s_e2r, {'tp': lax.rem(tp + k, n_tp)}).start()

        @pl.when(jnp.logical_or(r8 == 6, jnp.logical_and(r8 == 1, mc > 8)))
        def _():
            rc(DG.at[pl.ds(0, n_tp - 1)], DG.at[pl.ds(0, n_tp - 1)], s_e2s, s_e2r, to_partner).wait_recv()
            rc(DG.at[pl.ds(0, n_tp - 1)], DG.at[pl.ds(0, n_tp - 1)], s_e2s, s_e2r, to_partner).wait_send()
            rows = lax.broadcasted_iota(jnp.int32, (8, hd), 0)
            for k in range(n_tp):
                block = DG[k]
                for q in range(NQ):
                    part = block if q == 0 else pltpu.roll(block, 8 - 2 * q, axis=0)
                    cols = slice(k * SL + q * hd, k * SL + (q + 1) * hd)
                    DY[:, cols] = DY[:, cols] + jnp.where(rows < 2, part, 0.0)
            lq = lax.div(mc, 8)

            @pl.when(r8 == 6)
            def _():
                decode_norm(g2[pl.ds(lq, 1), :])

            @pl.when(jnp.logical_and(r8 == 1, mc < NS))
            def _():
                decode_norm(g1[pl.ds(jnp.minimum(lq, L - 1), 1), :])

        def decode_send():
            for k in range(n_tp):
                acc = DP[:, k * SL:k * SL + hd]
                for q in range(1, NQ):
                    acc = acc + pltpu.roll(DP[:, k * SL + q * hd:k * SL + (q + 1) * hd], 2 * q, axis=0)
                DS[k] = acc
            DR[tp] = DS[tp]
            for k in range(1, n_tp):
                to = lax.rem(tp + k, n_tp)
                rc(DS.at[to], DR.at[tp], s_e1s, s_e1r, {'tp': to}).start()

        par_c = lax.rem(mc, 2)
        sc = lax.rem(mc, STREAMS)
        lc_ = jnp.minimum(lax.div(mc, 8), L - 1)
        attn_c = jnp.logical_and(live_c, r8 < 4)
        mlp_c = jnp.logical_and(live_c, r8 >= 4)
        hi = lax.rem(sc, 2)
        pr_c = lax.div(sc, 2)

        for s in range(STREAMS):
            @pl.when(mc == s)
            def _():
                prompt_copy(s).wait()

                def first_rows(i, _):
                    rows = pl.ds(pl.multiple_of(i * BR, BR), BR)
                    hn = normed(H[s, rows, :].astype(F32), g1[0:1, :])
                    H[s, rows, :] = hn.astype(BF16)
                    return 0

                XR[s] = H[s, own_rows(X), :]
                lax.fori_loop(0, NB, first_rows, 0)

        @pl.when(attn_c)
        def _():
            @pl.when(sc == 0)
            def _():
                for w in wa_copies(lc_):
                    w.wait()

            c0 = 0
            while c0 < (G + 2) * hd:
                c1 = min(c0 + 2 * hd, (G + 2) * hd)
                QS[:, c0:c1] = jnp.dot(H[sc], WQ[:, c0:c1], preferred_element_type=F32).astype(BF16)
                c0 = c1
            rows = pl.ds(pl.multiple_of(hi * TS, TS), TS)
            for kv in range(2):
                KV[pr_c, kv, rows, :] = QS[0:TS, (G + kv) * hd:(G + kv + 1) * hd]

            @pl.when(hi == 1)
            def _():
                d_kv(lc_, pr_c).start()

            RT = tile_of(TS, 128)

            def attn_tile(i, _):
                g = lax.div(i, TS // RT)
                r = lax.rem(i, TS // RT)
                rows = pl.ds(pl.multiple_of(r * RT, RT), RT)
                cols = pl.ds(pl.multiple_of(g * hd, hd), hd)
                q = QS[rows, cols]
                scores = lax.dot_general(q, KV[pr_c, 0], (((1,), (1,)), ((), ())), preferred_element_type=F32) * scale
                qpos = hi * TS + r * RT + lax.broadcasted_iota(jnp.int32, (RT, T), 0)
                kpos = lax.broadcasted_iota(jnp.int32, (RT, T), 1)
                scores = jnp.where(qpos >= kpos, scores, -1e30)
                e = jnp.exp(scores - jnp.max(scores, axis=-1, keepdims=True))
                p = (e / jnp.sum(e, axis=-1, keepdims=True)).astype(BF16)
                OS[rows, cols] = jnp.dot(p, KV[pr_c, 1], preferred_element_type=F32).astype(BF16)
                return 0

            lax.fori_loop(0, G * (TS // RT), attn_tile, 0)

        UT = tile_of(F, 256)

        @pl.when(mlp_c)
        def _():
            @pl.when(sc == 0)
            def _():
                for w in wm_copies(lc_):
                    w.wait()

            def gate_up(i, _):
                cols = pl.ds(pl.multiple_of(i * UT, UT), UT)
                gate = jnp.dot(H[sc], WG[:, cols], preferred_element_type=F32)
                up = jnp.dot(H[sc], WU[:, cols], preferred_element_type=F32)
                US[:, cols] = (gate * (1.0 / (1.0 + jnp.exp(-gate))) * up).astype(BF16)
                return 0

            lax.fori_loop(0, F // UT, gate_up, 0)

        @pl.when(live_n)
        def _():
            for d in range(2):
                d_a(par_n, d).wait_recv()
                Y = Lf if d else R
                PB[par_n, d, Y, c] = PB[par_n, d, Y, c] + AR[par_n, d]
                d_c(par_n, d).start()

        NT = tile_of(DH, 512)

        def put(h, t, val):
            PB[par_c, h, :, :, :, pl.ds(pl.multiple_of(t * NT, NT), NT)] = (
                val[0:TS].astype(BF16).reshape(CHIPS, CORES, BR, NT))

        @pl.when(attn_c)
        def _():
            for h in range(2):
                def out_tile(t, _):
                    cols = pl.ds(pl.multiple_of(h * DH + t * NT, NT), NT)
                    put(h, t, jnp.dot(OS[...], WO[:, cols], preferred_element_type=F32))
                    return 0

                lax.fori_loop(0, DH // NT, out_tile, 0)
                d_pr(par_c, h).start()

        @pl.when(mlp_c)
        def _():
            for h in range(2):
                def down_tile(t, _):
                    cols = pl.ds(pl.multiple_of(h * DH + t * NT, NT), NT)
                    val = jnp.dot(US[...], WD[:, cols], preferred_element_type=F32)
                    put(h, t, val)
                    DP[:, cols] = val[TS:TS + 8]
                    return 0

                lax.fori_loop(0, DH // NT, down_tile, 0)
                d_pr(par_c, h).start()

        @pl.when(live_1)
        def _():
            s = lax.rem(m1, STREAMS)
            d_g(s, par_1, 0, 0).wait_recv()
            d_r(s, par_1, 0).start()
            d_g(s, par_1, 1, 1).wait_recv()
            d_r(s, par_1, 1).start()

        @pl.when(jnp.logical_and(live_c, r8 == 4))
        def _():
            for pr in range(2):
                d_kv(lc_, pr).wait_send()
            for pr in range(2):
                d_kv(lc_, pr).wait_recv()
            rows = lax.broadcasted_iota(jnp.int32, (DEC, hd), 0)
            outs = []
            for pr in range(2):
                for kv in range(2):
                    new = QS[TS:TS + DEC, (G + kv) * hd:(G + kv + 1) * hd].astype(F32)
                    new = jnp.sum(jnp.where(rows == pr, new, 0.0), axis=0, keepdims=True)
                    KVR[lc_, pr, kv, T:T + DEC, :] = jnp.where(rows == 0, new, 0.0).astype(BF16)
                q = jnp.concatenate([QS[TS:TS + DEC, g * hd:(g + 1) * hd] for g in range(G)], axis=0)
                scores = lax.dot_general(q, KVR[lc_, pr, 0], (((1,), (1,)), ((), ())), preferred_element_type=F32) * scale
                kpos = lax.broadcasted_iota(jnp.int32, (G * DEC, T + PAD), 1)
                scores = jnp.where(kpos <= T, scores, -1e30)
                e = jnp.exp(scores - jnp.max(scores, axis=-1, keepdims=True))
                p = (e / jnp.sum(e, axis=-1, keepdims=True)).astype(BF16)
                outs.append(jnp.dot(p, KVR[lc_, pr, 1], preferred_element_type=F32))
            picked = []
            for g in range(G):
                rest = jnp.where(rows == 1, outs[1][g * DEC:(g + 1) * DEC], 0.0)
                picked.append(jnp.where(rows == 0, outs[0][g * DEC:(g + 1) * DEC], rest).astype(BF16))
            od = jnp.concatenate(picked, axis=1)

            for t in range(D // NT):
                part = jnp.dot(od, WO[:, t * NT:(t + 1) * NT], preferred_element_type=F32)
                DP[:, t * NT:(t + 1) * NT] = part[0:8]
            decode_send()
            for pr in range(2):
                lc(KVR.at[lc_, pr, :, pl.ds(0, T + DEC)], (cb if pr else ca).at[lc_], s_ko.at[pr]).start()

            @pl.when(lax.div(mc, 8) + 1 < L)
            def _():
                for w in wa_copies(lax.div(mc, 8) + 1):
                    w.start()

        @pl.when(jnp.logical_and(live_c, r8 == 7))
        def _():
            decode_send()

            @pl.when(lax.div(mc, 8) + 1 < L)
            def _():
                for w in wm_copies(lax.div(mc, 8) + 1):
                    w.start()

        return 0

    lax.fori_loop(0, NS + 4, slot, 0)

    lc(DY, fin, s_fin).start()
    lc(DY, fin, s_fin).wait()
    for pr in range(2):
        lc(KVR.at[:, pr, :, pl.ds(0, T + DEC)], cb if pr else ca, s_ko.at[pr]).wait()
    for s in range(STREAMS):
        lc(H.at[s, pl.ds(0, TS)], (oa if s < 2 else ob).at[pl.ds((s % 2) * TS, TS)], s_out.at[s]).wait()


def device_specs():
    row_axes = ('pairs', 'ho')
    in_specs = (P('pairs', None, None), P('pairs', None, None), P(row_axes, None), P(row_axes, None),
                P(None, None, 'tp', None, None), P(None, 'tp', None, None, None), P(None, None, 'tp'),
                P(None, None, 'tp'), P(None, 'tp', None), P(None, None), P(None, None))
    out_specs = (P(row_axes, None, None), P(row_axes, None, None), P(row_axes, None), P(row_axes, None),
                 P(row_axes, None, None, None, 'tp', None), P(row_axes, None, None, None, 'tp', None))
    return in_specs, out_specs


def solution(mesh):
    n_ho, n_tp = mesh.shape['ho'], mesh.shape['tp']
    in_specs, out_specs = device_specs()

    def per_device(prompt_a, prompt_b, first_a, first_b, w_qkv, w_out, w_gate, w_up, w_down, norm_attn, norm_mlp):
        L, D = w_qkv.shape[0], w_qkv.shape[1]
        G, hd = w_out.shape[2], w_out.shape[3]
        F = w_gate.shape[2]
        T = prompt_a.shape[1]
        TS, DH = T // 2, D // 2
        BR = TS // n_tp
        wq = jnp.transpose(w_qkv[:, :, 0], (0, 2, 1, 3))
        wo = w_out.reshape(L, G * hd, D)
        y0 = jnp.concatenate([first_a, first_b, jnp.zeros((6, D), first_a.dtype)], axis=0).astype(F32)
        any_spec = pl.BlockSpec(memory_space=pl.ANY)
        vmem_spec = pl.BlockSpec(memory_space=pltpu.VMEM)
        dma = pltpu.SemaphoreType.DMA
        flops = 2 * L * 2 * T * D * (wq.shape[1] * hd + G * hd + 3 * F)
        outs = pl.pallas_call(
            functools.partial(body, (n_ho, n_tp, L, T, D, G, hd, F)),
            name='serve',
            out_shape=(
                jax.ShapeDtypeStruct((T, D), BF16), jax.ShapeDtypeStruct((T, D), BF16),
                jax.ShapeDtypeStruct((8, D), F32),
                jax.ShapeDtypeStruct((L, 2, T + DEC, hd), BF16), jax.ShapeDtypeStruct((L, 2, T + DEC, hd), BF16)),
            in_specs=[any_spec, any_spec, vmem_spec] + [any_spec] * 5 + [vmem_spec, vmem_spec],
            out_specs=(any_spec,) * 5,
            scratch_shapes=[
                pltpu.VMEM((STREAMS, TS + DEC, D), BF16),
                pltpu.VMEM((2, 2, CHIPS, CORES, BR, DH), BF16),
                pltpu.VMEM((2, 2, CHIPS, BR, DH), BF16),
                pltpu.VMEM((2, 2, BR, DH), BF16),
                pltpu.VMEM((2, 2, 2, BR, DH), BF16),
                pltpu.VMEM((STREAMS, BR, D), BF16),
                pltpu.VMEM((TS + DEC, (G + 2) * hd), BF16),
                pltpu.VMEM((2, 2, T, hd), BF16),
                pltpu.VMEM((TS, G * hd), BF16),
                pltpu.VMEM((TS + DEC, F), BF16),
                pltpu.VMEM((L, 2, 2, T + PAD, hd), BF16),
                pltpu.VMEM((D, (G + 2) * hd), BF16),
                pltpu.VMEM((G * hd, D), BF16),
                pltpu.VMEM((D, F), BF16),
                pltpu.VMEM((D, F), BF16),
                pltpu.VMEM((F, D), BF16),
                pltpu.VMEM((8, D), F32),
                pltpu.VMEM((8, D), F32),
                pltpu.VMEM((n_tp, 8, hd), F32),
                pltpu.VMEM((n_tp, 8, hd), F32),
                pltpu.VMEM((n_tp, 8, hd), F32),
                dma((2, 2)), dma((2, 2)),
                dma((2, 2)), dma((2, 2)),
                dma((2, 2)), dma((2, 2)),
                dma((2, 2)), dma((2, 2)),
                dma((2, 2, 2)), dma((2, 2, 2)),
                dma((2, 2)), dma((2, 2)),
                dma((STREAMS,)), dma((STREAMS,)),
                dma((2,)), dma((L, 2)),
                dma((G + 3,)), dma((3,)), dma((STREAMS,)), dma((STREAMS,)), dma((2,)),
                dma, dma, dma, dma, dma,
            ],
            compiler_params=pltpu.CompilerParams(
                collective_id=0, has_side_effects=True, vmem_limit_bytes=60 * 1024 * 1024),
            cost_estimate=pl.CostEstimate(flops=flops, bytes_accessed=2 * L * D * (5 * hd + G * hd + 3 * F), transcendentals=0),
        )(prompt_a, prompt_b, y0, wq, wo, w_gate, w_up, w_down, norm_attn, norm_mlp)
        out_a, out_b, fin, cache_a, cache_b = outs

        def cache(rows):
            return rows[:, :, :T + 1, None, :][None]

        return (out_a[None], out_b[None], fin[0:1], fin[1:2], cache(cache_a), cache(cache_b))

    return jax.shard_map(per_device, mesh=mesh, in_specs=in_specs, out_specs=out_specs, check_vma=False)
```

time: 2410 us -> 660 us (0.27)
  waiting for transfers between devices: 1270 us -> 0 us
  Pallas kernels: 0 us -> 644 us
  matrix products: 611 us -> 0 us
  blocking collectives: 289 us -> 0 us
  other arithmetic: 144 us -> 1.44 us
  between operations: 33.3 us -> 0.66 us
  local copies, waits for them, and re-layouts: 43.5 us -> 13.2 us
    psum x22 -> x0, waiting for transfers between devices: 1250 us -> none  [the longest x11 632 us: prefill_layer(): lax.psum(mlp_part, 'tp').astype(jnp.float32)]
    pallas_call x0 -> x1, Pallas kernels: none -> 644 us  [per_device(): pl.pallas_call(functools.partial(body, (n_ho, n_tp, L, T, D, G, hd, F)),...]
    dot_general x144 -> x0, matrix products: 611 us -> none  [the longest x12 166 us: prefill_layer(): jnp.dot(act_out, w_down, preferred_element_type=jnp.float32)]
    psum x12 -> x0, blocking collectives: 289 us -> none  [the longest x6 146 us: decode_layer(): dec_state = dec_state + lax.psum(attn_part, 'tp')]
    reduce_sum x67 -> x0, other arithmetic: 119 us -> none  [the longest x46 110 us: rms_norm(): jnp.mean(hidden_f * hidden_f, axis=-1, keepdims=True) + 1e-05]
  transfers between devices with their start and end apart: 24 -> 0, of which waited for: 22 -> 0; matrix products, arithmetic and copies ran while one was open for 12% -> 0% of each run, Pallas kernels for 0% -> 0%
where the time goes in v1:
time: 660 us; the launch traced here: 659 us
  Pallas kernels  644 us (98%)
  local copies, waits for them, and re-layouts  13.2 us (2%)
    pallas_call x1, Pallas kernels, per_device(): pl.pallas_call(functools.partial(body, (n_ho, n_tp, L, T, D, G, hd, F)),...  644 us

profile of v1, /device:TPU:97, one launch (start us, length us, event | category | flops | bytes accessed | tf_op | source)
XLA Modules:
  0.0 659.5 jit_solution(4459819467491315172)
XLA Ops:
  0.6 0.1 pad.2.clone
  0.7 1.4 maximum_convert_fusion.y0
  2.2 644.2 %serve.1 = (bf16[512,3072]{1,0:T(8,128)(2,1)}, bf16[512,3072]{1,0:T(8,128)(2,1)}, f32[8,3072]{1,0:T(8,128)}, bf16[6,2,528,128]{3,2,1,0:T(8,128)(2,1)}, bf16[6,2,528,128]{3,2,1,0:T(8,128)(2,1)}) custom-call(bf16[4,512,3072]{2,1,0:T(8,128)(2,1)} %pa.1, bf16[4,512,3072]{2,1,0:T(8,128)(2,1)} %pb.1, f32[8,3072]{1,0:T(8,128)} %maximum_convert_fusion.y0, ...), custom_call_target="tpu_custom_call" | custom-call | flops 154618822656 | bytes 150994944 | tf_op jit(solution)/shard_map/serve/pallas_call | solution.py:504
  646.4 1.6 fusion
  647.9 2.1 slice_bitcast_fusion
  650.1 0.0 copy-start.1
  650.1 2.4 copy.18
  652.4 2.4 copy.17
  654.8 0.0 copy-done.1
  654.8 0.0 copy-start
  654.8 1.7 copy.21
  656.5 1.4 copy-done
  657.8 1.7 copy.22
  (1 shorter events, 0.0 us)
Async XLA Ops:
  650.1 4.7 copy-start.1
  654.8 3.0 copy-start

commit v2 on v1

--- a/solution.py
+++ b/solution.py
@@ -24,18 +24,17 @@
     return tile
 
 
-def body(cfg, pa, pb, y0, wq, wo, wg, wu, wd, g1, g2, oa, ob, fin, ca, cb,
-         H, PB, PR, AR, BC, XR, QS, KV, OS, US, KVR, WQ, WO, WG, WU, WD, DY, DP, DS, DR, DG,
+def body(cfg, pa, pb, fa, fb, wq, wo, wg, wu, wd, g1, g2, oa, ob, fin_a, fin_b, ca, cb,
+         H, PB, PR, AR, BC, XR, QS, KV, OS, US, KVR, WQ, WO, WG, WU, WD, DY, DP, EX, Z32, ZB,
          s_prs, s_prr, s_as, s_ar, s_bs, s_br, s_cs, s_cr, s_gs, s_gr, s_rs, s_rr, s_ds, s_dr,
-         s_kvs, s_kvr, s_wa, s_wm, s_in, s_out, s_ko, s_e1s, s_e1r, s_e2s, s_e2r, s_fin):
+         s_kvs, s_kvr, s_wa, s_wm, s_in, s_out, s_ko, s_es, s_er):
     n_ho, n_tp, L, T, D, G, hd, F = cfg
     TS = T // 2
     NB = n_tp
     BR = TS // NB
     DH = D // 2
     NS = 8 * L
-    SL = D // n_tp
-    NQ = SL // hd
+    NT4 = EX.shape[1]
     scale = hd ** -0.5
     j = lax.axis_index('ho')
     tp = lax.axis_index('tp')
@@ -94,6 +93,18 @@
     def d_kv(l, pr):
         return rc(KV.at[pr], KVR.at[l, pr, :, pl.ds(0, T)], s_kvs.at[pr], s_kvr.at[l, pr], {'ho': ho_right})
 
+    first_pair = {'tp': (X + 1 - 2 * lax.rem(X, 2)) * CORES + c}
+    second_pair = {'tp': (CHIPS - 1 - X) * CORES + c}
+    E_OUT, E_IN0, E_A, E_IN1, E_B, E_IN2, E_C, E_IN3 = range(8)
+
+    def d_e(step):
+        src, dst, dev = ((E_OUT, E_IN0, to_partner), (E_A, E_IN1, first_pair), (E_B, E_IN2, second_pair),
+                         (E_C, E_IN3, to_partner))[step]
+        return rc(EX.at[src], EX.at[dst], s_es.at[step], s_er.at[step], dev)
+
+    def cache_copy(l, pr):
+        return lc(ZB.at[pr, pl.ds(0, T + 1)], (cb if pr else ca).at[pl.ds(l * (T + 1), T + 1)], s_ko.at[pr])
+
     def wa_copies(l):
         out = [lc(wq.at[l, i], WQ.at[:, pl.ds(i * hd, hd)], s_wa.at[i]) for i in range(G + 2)]
         return out + [lc(wo.at[l], WO, s_wa.at[G + 2])]
@@ -114,10 +125,6 @@
     prompt_copy(0).start()
     for w in wa_copies(0):
         w.start()
-    for s in range(1, STREAMS):
-        prompt_copy(s).start()
-    for w in wm_copies(0):
-        w.start()
     KV[...] = jnp.zeros(KV.shape, BF16)
     for s in range(STREAMS):
         H[s, TS:TS + DEC, :] = jnp.zeros((DEC, D), BF16)
@@ -138,7 +145,9 @@
         h = normed(DY[...], gain)
         H[STREAMS - 1, TS:TS + DEC, :] = jnp.concatenate([h, jnp.zeros_like(h)], axis=0).astype(BF16)
 
-    DY[...] = y0[...]
+    DY[...] = jnp.zeros(DY.shape, F32)
+    DY[0:1, :] = fa[...].astype(F32)
+    DY[1:2, :] = fb[...].astype(F32)
     decode_norm(g1[0:1, :])
     pl.semaphore_wait(barrier, n_tp - 1 + 2)
 
@@ -245,49 +254,54 @@
                 lc(H.at[s, pl.ds(0, TS)], (oa if s < 2 else ob).at[pl.ds((s % 2) * TS, TS)], s_out.at[s]).start()
 
         r8 = lax.rem(mc, 8)
+        rows8 = lax.broadcasted_iota(jnp.int32, (8, hd), 0)
+
+        def half_cols(half, k):
+            return pl.ds(pl.multiple_of(half * DH + k * hd, hd), hd)
+
+        def decode_send():
+            for slot_, half in ((E_OUT, 1 - c), (E_A, c)):
+                for t in range(NT4):
+                    acc = DP[:, half_cols(half, 4 * t)]
+                    for q in range(1, 4):
+                        acc = acc + pltpu.roll(DP[:, half_cols(half, 4 * t + q)], 2 * q, axis=0)
+                    EX[slot_, t] = acc
+            d_e(0).start()
 
         @pl.when(jnp.logical_or(r8 == 5, jnp.logical_and(r8 == 0, mc > 0)))
         def _():
-            rc(DS.at[pl.ds(0, n_tp - 1)], DR.at[pl.ds(0, n_tp - 1)], s_e1s, s_e1r, to_partner).wait_recv()
-            rc(DS.at[pl.ds(0, n_tp - 1)], DR.at[pl.ds(0, n_tp - 1)], s_e1s, s_e1r, to_partner).wait_send()
-            acc = DR[0]
-            for k in range(1, n_tp):
-                acc = acc + DR[k]
-            DG[tp] = acc
-            for k in range(1, n_tp):
-                rc(DG.at[tp], DG.at[tp], s_e2s, s_e2r, {'tp': lax.rem(tp + k, n_tp)}).start()
+            d_e(0).wait_recv()
+            d_e(0).wait_send()
+            EX[E_A] = EX[E_A] + EX[E_IN0]
+            d_e(1).start()
 
         @pl.when(jnp.logical_or(r8 == 6, jnp.logical_and(r8 == 1, mc > 8)))
         def _():
-            rc(DG.at[pl.ds(0, n_tp - 1)], DG.at[pl.ds(0, n_tp - 1)], s_e2s, s_e2r, to_partner).wait_recv()
-            rc(DG.at[pl.ds(0, n_tp - 1)], DG.at[pl.ds(0, n_tp - 1)], s_e2s, s_e2r, to_partner).wait_send()
-            rows = lax.broadcasted_iota(jnp.int32, (8, hd), 0)
-            for k in range(n_tp):
-                block = DG[k]
-                for q in range(NQ):
-                    part = block if q == 0 else pltpu.roll(block, 8 - 2 * q, axis=0)
-                    cols = slice(k * SL + q * hd, k * SL + (q + 1) * hd)
-                    DY[:, cols] = DY[:, cols] + jnp.where(rows < 2, part, 0.0)
+            d_e(2).wait_recv()
+            d_e(2).wait_send()
+            EX[E_C] = EX[E_B] + EX[E_IN2]
+            d_e(3).start()
+
+        @pl.when(jnp.logical_or(r8 == 7, jnp.logical_and(r8 == 2, mc > 8)))
+        def _():
+            d_e(3).wait_recv()
+            d_e(3).wait_send()
+            for slot_, half in ((E_C, c), (E_IN3, 1 - c)):
+                for t in range(NT4):
+                    block = EX[slot_, t]
+                    for q in range(4):
+                        part = block if q == 0 else pltpu.roll(block, 8 - 2 * q, axis=0)
+                        cols = half_cols(half, 4 * t + q)
+                        DY[:, cols] = DY[:, cols] + jnp.where(rows8 < 2, part, 0.0)
             lq = lax.div(mc, 8)
 
-            @pl.when(r8 == 6)
+            @pl.when(r8 == 7)
             def _():
                 decode_norm(g2[pl.ds(lq, 1), :])
 
-            @pl.when(jnp.logical_and(r8 == 1, mc < NS))
+            @pl.when(jnp.logical_and(r8 == 2, mc < NS))
             def _():
                 decode_norm(g1[pl.ds(jnp.minimum(lq, L - 1), 1), :])
-
-        def decode_send():
-            for k in range(n_tp):
-                acc = DP[:, k * SL:k * SL + hd]
-                for q in range(1, NQ):
-                    acc = acc + pltpu.roll(DP[:, k * SL + q * hd:k * SL + (q + 1) * hd], 2 * q, axis=0)
-                DS[k] = acc
-            DR[tp] = DS[tp]
-            for k in range(1, n_tp):
-                to = lax.rem(tp + k, n_tp)
-                rc(DS.at[to], DR.at[tp], s_e1s, s_e1r, {'tp': to}).start()
 
         par_c = lax.rem(mc, 2)
         sc = lax.rem(mc, STREAMS)
@@ -317,6 +331,13 @@
             def _():
                 for w in wa_copies(lc_):
                     w.wait()
+
+                @pl.when(mc == 0)
+                def _():
+                    for s in range(1, STREAMS):
+                        prompt_copy(s).start()
+                    for w in wm_copies(0):
+                        w.start()
 
             c0 = 0
             while c0 < (G + 2) * hd:
@@ -414,6 +435,13 @@
             d_g(s, par_1, 1, 1).wait_recv()
             d_r(s, par_1, 1).start()
 
+        @pl.when(jnp.logical_or(r8 == 5, jnp.logical_and(r8 == 0, mc > 0)))
+        def _():
+            d_e(1).wait_recv()
+            d_e(1).wait_send()
+            EX[E_B] = EX[E_A] + EX[E_IN1]
+            d_e(2).start()
+
         @pl.when(jnp.logical_and(live_c, r8 == 4))
         def _():
             for pr in range(2):
@@ -423,10 +451,20 @@
             rows = lax.broadcasted_iota(jnp.int32, (DEC, hd), 0)
             outs = []
             for pr in range(2):
+                @pl.when(lc_ > 0)
+                def _():
+                    cache_copy(lc_ - 1, pr).wait()
+
+                both = jnp.zeros((DEC, hd), F32)
                 for kv in range(2):
                     new = QS[TS:TS + DEC, (G + kv) * hd:(G + kv + 1) * hd].astype(F32)
                     new = jnp.sum(jnp.where(rows == pr, new, 0.0), axis=0, keepdims=True)
                     KVR[lc_, pr, kv, T:T + DEC, :] = jnp.where(rows == 0, new, 0.0).astype(BF16)
+                    both = jnp.where(rows == kv, new, both)
+                    Z32[pl.ds(kv, T, stride=2), :] = KVR[lc_, pr, kv, 0:T, :].astype(F32)
+                ZB[pr, 0:T] = Z32[...].astype(BF16).reshape(T, 2, hd)
+                ZB[pr, T:T + DEC // 2] = both.astype(BF16).reshape(DEC // 2, 2, hd)
+                cache_copy(lc_, pr).start()
                 q = jnp.concatenate([QS[TS:TS + DEC, g * hd:(g + 1) * hd] for g in range(G)], axis=0)
                 scores = lax.dot_general(q, KVR[lc_, pr, 0], (((1,), (1,)), ((), ())), preferred_element_type=F32) * scale
                 kpos = lax.broadcasted_iota(jnp.int32, (G * DEC, T + PAD), 1)
@@ -444,8 +482,6 @@
                 part = jnp.dot(od, WO[:, t * NT:(t + 1) * NT], preferred_element_type=F32)
                 DP[:, t * NT:(t + 1) * NT] = part[0:8]
             decode_send()
-            for pr in range(2):
-                lc(KVR.at[lc_, pr, :, pl.ds(0, T + DEC)], (cb if pr else ca).at[lc_], s_ko.at[pr]).start()
 
             @pl.when(lax.div(mc, 8) + 1 < L)
             def _():
@@ -465,10 +501,10 @@
 
     lax.fori_loop(0, NS + 4, slot, 0)
 
-    lc(DY, fin, s_fin).start()
-    lc(DY, fin, s_fin).wait()
+    fin_a[...] = DY[0:1, :]
+    fin_b[...] = DY[1:2, :]
     for pr in range(2):
-        lc(KVR.at[:, pr, :, pl.ds(0, T + DEC)], cb if pr else ca, s_ko.at[pr]).wait()
+        cache_copy(L - 1, pr).wait()
     for s in range(STREAMS):
         lc(H.at[s, pl.ds(0, TS)], (oa if s < 2 else ob).at[pl.ds((s % 2) * TS, TS)], s_out.at[s]).wait()
 
@@ -496,7 +532,6 @@
         BR = TS // n_tp
         wq = jnp.transpose(w_qkv[:, :, 0], (0, 2, 1, 3))
         wo = w_out.reshape(L, G * hd, D)
-        y0 = jnp.concatenate([first_a, first_b, jnp.zeros((6, D), first_a.dtype)], axis=0).astype(F32)
         any_spec = pl.BlockSpec(memory_space=pl.ANY)
         vmem_spec = pl.BlockSpec(memory_space=pltpu.VMEM)
         dma = pltpu.SemaphoreType.DMA
@@ -506,10 +541,10 @@
             name='serve',
             out_shape=(
                 jax.ShapeDtypeStruct((T, D), BF16), jax.ShapeDtypeStruct((T, D), BF16),
-                jax.ShapeDtypeStruct((8, D), F32),
-                jax.ShapeDtypeStruct((L, 2, T + DEC, hd), BF16), jax.ShapeDtypeStruct((L, 2, T + DEC, hd), BF16)),
-            in_specs=[any_spec, any_spec, vmem_spec] + [any_spec] * 5 + [vmem_spec, vmem_spec],
-            out_specs=(any_spec,) * 5,
+                jax.ShapeDtypeStruct((1, D), F32), jax.ShapeDtypeStruct((1, D), F32),
+                jax.ShapeDtypeStruct((L * (T + 1), 2, hd), BF16), jax.ShapeDtypeStruct((L * (T + 1), 2, hd), BF16)),
+            in_specs=[any_spec] * 2 + [vmem_spec] * 2 + [any_spec] * 5 + [vmem_spec] * 2,
+            out_specs=(any_spec, any_spec, vmem_spec, vmem_spec, any_spec, any_spec),
             scratch_shapes=[
                 pltpu.VMEM((STREAMS, TS + DEC, D), BF16),
                 pltpu.VMEM((2, 2, CHIPS, CORES, BR, DH), BF16),
@@ -529,9 +564,9 @@
                 pltpu.VMEM((F, D), BF16),
                 pltpu.VMEM((8, D), F32),
                 pltpu.VMEM((8, D), F32),
-                pltpu.VMEM((n_tp, 8, hd), F32),
-                pltpu.VMEM((n_tp, 8, hd), F32),
-                pltpu.VMEM((n_tp, 8, hd), F32),
+                pltpu.VMEM((8, DH // (4 * hd), 8, hd), F32),
+                pltpu.VMEM((2 * T, hd), F32),
+                pltpu.VMEM((2, T + 8, 2, hd), BF16),
                 dma((2, 2)), dma((2, 2)),
                 dma((2, 2)), dma((2, 2)),
                 dma((2, 2)), dma((2, 2)),
@@ -541,17 +576,17 @@
                 dma((STREAMS,)), dma((STREAMS,)),
                 dma((2,)), dma((L, 2)),
                 dma((G + 3,)), dma((3,)), dma((STREAMS,)), dma((STREAMS,)), dma((2,)),
-                dma, dma, dma, dma, dma,
+                dma((4,)), dma((4,)),
             ],
             compiler_params=pltpu.CompilerParams(
-                collective_id=0, has_side_effects=True, vmem_limit_bytes=60 * 1024 * 1024),
+                collective_id=0, has_side_effects=True, vmem_limit_bytes=44 * 1024 * 1024),
             cost_estimate=pl.CostEstimate(flops=flops, bytes_accessed=2 * L * D * (5 * hd + G * hd + 3 * F), transcendentals=0),
-        )(prompt_a, prompt_b, y0, wq, wo, w_gate, w_up, w_down, norm_attn, norm_mlp)
-        out_a, out_b, fin, cache_a, cache_b = outs
+        )(prompt_a, prompt_b, first_a, first_b, wq, wo, w_gate, w_up, w_down, norm_attn, norm_mlp)
+        out_a, out_b, fin_a, fin_b, cache_a, cache_b = outs
 
         def cache(rows):
-            return rows[:, :, :T + 1, None, :][None]
-
-        return (out_a[None], out_b[None], fin[0:1], fin[1:2], cache(cache_a), cache(cache_b))
+            return jnp.transpose(rows.reshape(L, T + 1, 2, hd), (0, 2, 1, 3))[None, :, :, :, None, :]
+
+        return (out_a[None], out_b[None], fin_a, fin_b, cache(cache_a), cache(cache_b))
 
     return jax.shard_map(per_device, mesh=mesh, in_specs=in_specs, out_specs=out_specs, check_vma=False)

time: 660 us -> 645 us (0.977)
  Pallas kernels: 644 us -> 634 us
    pallas_call x1, Pallas kernels: 644 us -> 634 us  [per_device(): pl.pallas_call(functools.partial(body, (n_ho, n_tp, L, T, D, G, hd, F)),...]
where the time goes in v2:
time: 645 us
  Pallas kernels  634 us (98%)
  local copies, waits for them, and re-layouts  10 us (2%)
    pallas_call x1, Pallas kernels, per_device(): pl.pallas_call(functools.partial(body, (n_ho, n_tp, L, T, D, G, hd, F)),...  634 us

profile of v2, /device:TPU:97, one launch (start us, length us, event | category | flops | bytes accessed | tf_op | source)
XLA Modules:
  0.0 644.6 jit_solution(8100752294318688709)
XLA Ops:
  0.6 0.0 copy-start
  0.6 0.9 copy-done
  1.5 0.0 copy-start.1
  1.5 0.9 copy-done.1
  2.4 0.0 copy-start.2
  2.4 0.7 copy-done.2
  3.1 0.0 copy-start.3
  3.1 0.7 copy-done.3
  3.8 634.0 %serve.1 = (bf16[512,3072]{1,0:T(8,128)(2,1)S(1)}, bf16[512,3072]{1,0:T(8,128)(2,1)S(1)}, f32[1,3072]{1,0:T(1,128)S(1)}, f32[1,3072]{1,0:T(1,128)S(1)}, bf16[307...) custom-call(bf16[4,512,3072]{2,1,0:T(8,128)(2,1)} %pa.1, bf16[4,512,3072]{2,1,0:T(8,128)(2,1)} %pb.1, ...), custom_call_target="tpu_custom_call" | custom-call | flops 154618822656 | bytes 150994944 | tf_op jit(solution)/shard_map/serve/pallas_call | solution.py:539
  637.8 1.7 copy.23
  639.5 1.7 copy.24
  641.2 0.6 copy.25
  641.8 0.6 copy.26
  642.4 1.1 copy.27
  643.5 1.1 copy.28
Async XLA Ops:
  0.6 0.9 copy-start
  1.5 0.9 copy-start.1
  2.4 0.7 copy-start.2
  3.1 0.7 copy-start.3

commit v3 on v2

v3 whole, which is shorter than its diff:
```python
import functools

import jax
import jax.numpy as jnp
from jax import lax
from jax.experimental import pallas as pl
from jax.experimental.pallas import tpu as pltpu
from jax.sharding import PartitionSpec as P

MESH = pl.DeviceIdType.MESH
F32 = jnp.float32
BF16 = jnp.bfloat16
CORES = 2
CHIPS = 4
STREAMS = 4
DEC = 16
PAD = 128


def tile_of(size, most):
    tile = most
    while size % tile:
        tile //= 2
    return tile


def body(cfg, pa, pb, fa, fb, wq, wo, wg, wu, wd, g1h, g2h, oa, ob, fin_a, fin_b, ca, cb, fq, fo,
         H, PB, PR, AR, BC, XR, QS, KV, OS, US, KVR, WQ, WO, WQF, WOF, WG, WU, WD, g1, g2, FT, DY, DP, EX, Z32, ZB,
         s_prs, s_prr, s_as, s_ar, s_bs, s_br, s_cs, s_cr, s_gs, s_gr, s_rs, s_rr, s_ds, s_dr,
         s_kvs, s_kvr, s_wa, s_wf, s_wm, s_in, s_out, s_ko, s_es, s_er, s_sm,
         s_xs, s_xr, s_us, s_ur, s_ls, s_lr, s_ys, s_yr, s_sync):
    n_ho, n_tp, L, T, D, G, hd, F = cfg
    TS = T // 2
    HS = TS // 2
    BR = TS // n_tp
    DH = D // 2
    NS = 8 * L
    NT4 = EX.shape[1]
    DQ = D // n_ho
    OQ = G * hd // n_ho
    OC = OQ // 3
    scale = hd ** -0.5
    j = lax.axis_index('ho')
    tp = lax.axis_index('tp')
    X = lax.div(tp, CORES)
    c = lax.rem(tp, CORES)
    Q = CHIPS - 1 - X
    V = X + 1 - 2 * lax.rem(X, 2)
    O = CHIPS - 1 - V
    near = (Q, V)

    def pos(Y):
        return 2 * lax.rem(lax.div(Y + 1, 2), 2) + lax.div(Y, 2)

    pX, pQ, pV, pO = pos(X), pos(Q), pos(V), pos(O)
    pN = (pQ, pV)
    hp = lax.div(pX, 2)
    to_near = ({'tp': Q * CORES + c}, {'tp': V * CORES + c})
    to_partner = {'tp': X * CORES + (1 - c)}
    up = lax.rem(j + 1, n_ho)
    down = lax.rem(j + n_ho - 1, n_ho)

    def rc(src, dst, ss, rs, dev):
        return pltpu.make_async_remote_copy(src_ref=src, dst_ref=dst, send_sem=ss, recv_sem=rs,
                                            device_id=dev, device_id_type=MESH)

    def lc(src, dst, sem):
        return pltpu.make_async_copy(src, dst, sem)

    def rows_of(p):
        return pl.ds(pl.multiple_of((p * CORES + c) * BR, BR), BR)

    def d_pr(par, h):
        return rc(PB.at[par, h, :, 1 - c], PR.at[par, h], s_prs.at[par, h], s_prr.at[par, h], to_partner)

    def d_pr_home(par, h):
        return rc(PB.at[par, h, pl.ds(hp * 2, 2), 1 - c], PR.at[par, h, pl.ds(hp * 2, 2)],
                  s_prs.at[par, h], s_prr.at[par, h], to_partner)

    def d_a(par, e, heavy=False):
        return rc(PB.at[par, e, pO, c], AR.at[par, e], s_as.at[par, e], s_ar.at[par, e], to_near[0 if heavy else e])

    def d_b(par, s, e):
        return rc(PB.at[par, e, pN[e], c], BC.at[s, e, e], s_bs.at[s, e], s_br.at[s, e], to_near[e])

    def d_c(par, s, e):
        return rc(PB.at[par, 1 - e, pN[e], c], BC.at[s, e, 1 - e], s_cs.at[s, e], s_cr.at[s, e], to_near[e])

    def h_part(s, p, half):
        return H.at[s, rows_of(p), pl.ds(half * DH, DH)]

    def d_g(s, par, e, half):
        return rc(h_part(s, pX, half), h_part(s, pX, half), s_gs.at[par, e, half], s_gr.at[par, e, half], to_near[e])

    def d_r(s, par, e):
        return rc(h_part(s, pN[e], e), h_part(s, pN[e], e), s_rs.at[par, e], s_rr.at[par, e], to_near[1 - e])

    def d_d(s, p):
        return rc(H.at[s, rows_of(p)], H.at[s, rows_of(p)], s_ds.at[s], s_dr.at[s], to_partner)

    def d_d_all(s, blocks):
        return rc(H.at[s, pl.ds(0, blocks * BR)], H.at[s, pl.ds(0, blocks * BR)], s_ds.at[s], s_dr.at[s], to_partner)

    def quarter(s):
        return pl.ds(pl.multiple_of(s * HS, HS), HS)

    def d_kv(l, f, pr, s, dev):
        return rc(KV.at[f, :, quarter(s)], KVR.at[l, pr, :, quarter(s)], s_kvs.at[f], s_kvr.at[l, pr], dev)

    def d_kv_all(l, f, pr):
        return rc(KV.at[f], KVR.at[l, pr, :, pl.ds(0, T)], s_kvs.at[f], s_kvr.at[l, pr], to_partner)

    E_OUT, E_IN0, E_A, E_IN1, E_B, E_IN2, E_C, E_IN3 = range(8)

    def d_e(step):
        src, dst, dev = ((E_OUT, E_IN0, to_partner), (E_A, E_IN1, to_near[1]), (E_B, E_IN2, to_near[0]),
                         (E_C, E_IN3, to_partner))[step]
        return rc(EX.at[src], EX.at[dst], s_es.at[step], s_er.at[step], dev)

    def cache_copy(l, pr):
        return lc(ZB.at[pr, pl.ds(0, T + 1)], (cb if pr else ca).at[pl.ds(l * (T + 1), T + 1)], s_ko.at[pr])

    def piece(refs, l, k, wide, r):
        if wide:
            return refs[0].at[l, k, pl.ds(pl.multiple_of(r * DQ, DQ), DQ), :]
        return refs[1].at[l, pl.ds(pl.multiple_of(r * OQ + (k - (G + 2)) * OC, OC), OC), :]

    def d_x(l, k, wide):
        return rc(piece((wq, wo), l, k, wide, j), piece((fq, fo), l - 1, k, wide, j), s_xs.at[k], s_xr.at[k], to_near[1])

    def d_up(l, k, wide, r):
        ref = piece((fq, fo), l - 1, k, wide, r)
        return rc(ref, ref, s_us.at[k], s_ur.at[k], {'ho': up})

    def d_down(l, k, wide, r):
        ref = piece((fq, fo), l - 1, k, wide, r)
        return rc(ref, ref, s_ls.at[k], s_lr.at[k], {'ho': down})

    def d_on(l, k, wide, r, dev):
        ref = piece((fq, fo), l - 1, k, wide, r)
        return rc(ref, ref, s_ys.at[k], s_yr.at[k], dev)

    def wa_copies(l):
        out = [lc(wq.at[l, i], WQ.at[:, pl.ds(i * hd, hd)], s_wa.at[i]) for i in range(G + 2)]
        return out + [lc(wo.at[l], WO, s_wa.at[G + 2])]

    def wf_copies(l):
        out = [lc(fq.at[l - 1, i], WQF.at[:, pl.ds(i * hd, hd)], s_wf.at[i]) for i in range(G + 2)]
        return out + [lc(fo.at[l - 1], WOF, s_wf.at[G + 2])]

    def wm_copies(l):
        return [lc(wg.at[l], WG, s_wm.at[0]), lc(wu.at[l], WU, s_wm.at[1]), lc(wd.at[l], WD, s_wm.at[2])]

    def prompt_copies(s):
        return [lc(p.at[j, pl.ds(s * HS, HS)], H.at[s, pl.ds(i * HS, HS)], s_in.at[s, i]) for i, p in enumerate((pa, pb))]

    def out_copies(s):
        return [lc(H.at[s, pl.ds(i * HS, HS)], o.at[pl.ds(s * HS, HS)], s_out.at[s, i]) for i, o in enumerate((oa, ob))]

    small = [lc(g1h, g1, s_sm.at[0]), lc(g2h, g2, s_sm.at[1]), lc(fa, FT.at[0], s_sm.at[2]), lc(fb, FT.at[1], s_sm.at[3])]

    barrier = pltpu.get_barrier_semaphore()
    met = [to_partner, to_near[0], to_near[1], {'ho': up}, {'ho': down},
           {'ho': up, 'tp': V * CORES + c}, {'ho': down, 'tp': V * CORES + c}]
    for dev in met:
        pl.semaphore_signal(barrier, inc=1, device_id=dev, device_id_type=MESH)

    for w in prompt_copies(0) + small + wa_copies(0):
        w.start()
    KV[...] = jnp.zeros(KV.shape, BF16)
    for s in range(STREAMS):
        H[s, TS:TS + DEC, :] = jnp.zeros((DEC, D), BF16)

    def zero_kvr(l, _):
        for pr in range(2):
            for kv in range(2):
                KVR[l, pr, kv, T:T + PAD, :] = jnp.zeros((PAD, hd), BF16)
        return 0

    lax.fori_loop(0, L, zero_kvr, 0)

    def normed(xf, gain):
        ms = jnp.mean(xf * xf, axis=-1, keepdims=True)
        return xf * lax.rsqrt(ms + 1e-5) * gain

    def decode_norm(gain):
        h = normed(DY[...], gain)
        H[STREAMS - 1, TS:TS + DEC, :] = jnp.concatenate([h, jnp.zeros_like(h)], axis=0).astype(BF16)

    for w in small:
        w.wait()
    DY[...] = jnp.zeros(DY.shape, F32)
    DY[0:1, :] = FT[0].astype(F32)
    DY[1:2, :] = FT[1].astype(F32)
    decode_norm(g1[0:1, :])
    pl.semaphore_wait(barrier, len(met))

    def slot(it, _):
        n = it - 1
        m1, m2, m3, mc = n - 1, n - 2, n - 3, n + 1

        def state(m):
            live = jnp.logical_and(m >= 0, m < NS)
            r = lax.rem(m + 16, 8)
            full_rs = jnp.logical_or(m < 8, r >= 4)
            full_ag = jnp.logical_or(r < 4, m >= NS - STREAMS)
            return live, full_rs, full_ag

        def when(*conds):
            out = conds[0]
            for x in conds[1:]:
                out = jnp.logical_and(out, x)
            return pl.when(out)

        live_n, frs_n, _ = state(n)
        live_1, frs_1, fag_1 = state(m1)
        live_2, _, fag_2 = state(m2)
        live_3, _, fag_3 = state(m3)
        live_c, frs_c, _ = state(mc)
        heavy = jnp.logical_and(n >= 1, n < STREAMS)
        par_n, par_1 = lax.rem(n + 8, 2), lax.rem(m1 + 8, 2)
        s_n, s_1, s_2, s_3 = (lax.rem(m + 8, STREAMS) for m in (n, m1, m2, m3))

        def add(h, p):
            PB[par_n, h, p, c] = PB[par_n, h, p, c] + PR[par_n, h, p]

        @when(live_n, frs_n)
        def _():
            for h in range(2):
                d_pr(par_n, h).wait_recv()
            for e in range(2):
                add(e, pO)

            @when(jnp.logical_not(heavy))
            def _():
                for e in range(2):
                    d_a(par_n, e).start()
                for e in range(2):
                    add(e, pN[e])
                for e in range(2):
                    d_b(par_n, s_n, e).start()
                for e in range(2):
                    add(1 - e, pN[e])

            @when(heavy)
            def _():
                for e in range(2):
                    d_a(par_n, e, True).start()
                for e in range(2):
                    add(e, pQ)
                d_b(par_n, s_n, 0).start()
                d_c(par_n, s_n, 0).start()
                for e in range(2):
                    add(e, pV)

            for e in range(2):
                add(e, pX)

        @when(live_n, jnp.logical_not(frs_n))
        def _():
            for h in range(2):
                d_pr_home(par_n, h).wait_recv()
            for h in range(2):
                add(h, pQ)
            d_b(par_n, s_n, 0).start()
            d_c(par_n, s_n, 0).start()
            for h in range(2):
                add(h, pX)

        def pieces(t, fn):
            r = lax.rem(t + 8, 8)

            @when(t == -1)
            def _():
                for k in range(3):
                    fn(1, k, True)

            @when(t >= 0, r == 0, lax.div(t, 8) + 1 < L)
            def _():
                for k in (3, 4):
                    fn(lax.div(t, 8) + 1, k, True)

            @when(t >= 0, r >= 1, r <= 3, lax.div(t, 8) + 1 < L)
            def _():
                fn(lax.div(t, 8) + 1, 4 + r, False)

            @when(t >= 0, r >= 5, lax.div(t, 8) + 2 < L)
            def _():
                fn(lax.div(t, 8) + 2, r - 5, True)

        pieces(n, lambda l, k, wide: d_x(l, k, wide).start())

        @when(n >= 0)
        def _():
            for e in range(2):
                pl.semaphore_wait(s_sync.at[e], 1)

        @when(live_1)
        def _():
            l = lax.div(m1, 8)
            is_attn = lax.rem(lax.div(m1, 4), 2) == 0
            last = m1 >= NS - STREAMS
            d_b(par_1, s_1, 0).wait_recv()
            d_c(par_1, s_1, 0).wait_recv()

            @when(frs_1)
            def _():
                d_b(par_1, s_1, 1).wait_recv()
                d_c(par_1, s_1, 1).wait_recv()

            x_new = []
            ms = jnp.zeros((BR, 1), F32)
            for h in range(2):
                second = jnp.where(frs_1, BC[s_1, 1, h].astype(F32), 0.0)
                total = PB[par_1, h, pX, c].astype(F32) + (BC[s_1, 0, h].astype(F32) + second)
                cols = slice(h * DH, (h + 1) * DH)
                x = XR[s_1, :, cols].astype(F32) + total.astype(BF16).astype(F32)
                x = x.astype(BF16)
                XR[s_1, :, cols] = x
                x = x.astype(F32)
                ms = ms + jnp.sum(x * x, axis=-1, keepdims=True)
                x_new.append(x)
            inv = lax.rsqrt(ms * (1.0 / D) + 1e-5)
            nl = jnp.minimum(l + 1, L - 1)
            for h in range(2):
                cols = slice(h * DH, (h + 1) * DH)
                gain = jnp.where(is_attn, g2[pl.ds(l, 1), cols], g1[pl.ds(nl, 1), cols])
                hn = x_new[h] * inv * gain
                H[s_1, rows_of(pX), cols] = jnp.where(last, x_new[h], hn).astype(BF16)

            d_g(s_1, par_1, 0, 0).start()

            @when(fag_1)
            def _():
                d_g(s_1, par_1, 1, 1).start()

            d_g(s_1, par_1, 0, 1).start()

            @when(fag_1)
            def _():
                d_g(s_1, par_1, 1, 0).start()

            d_d(s_1, pX).start()

        @when(live_1)
        def _():
            d_b(par_1, s_1, 0).wait_send()
            d_c(par_1, s_1, 0).wait_send()

            @when(frs_1)
            def _():
                for h in range(2):
                    d_pr(par_1, h).wait_send()
                for e in range(2):
                    d_a(par_1, e).wait_send()
                d_b(par_1, s_1, 1).wait_send()
                d_c(par_1, s_1, 1).wait_send()

            @when(jnp.logical_not(frs_1))
            def _():
                for h in range(2):
                    d_pr_home(par_1, h).wait_send()

        @when(live_2)
        def _():
            par = lax.rem(m2, 2)
            d_g(s_2, par, 0, 1).wait_recv()

            @when(jnp.logical_not(fag_2))
            def _():
                d_g(s_2, par, 0, 0).wait_recv()

            d_d(s_2, pQ).start()

            @when(fag_2)
            def _():
                d_g(s_2, par, 1, 0).wait_recv()
                d_d(s_2, pV).start()
                for e in range(2):
                    d_r(s_2, par, e).wait_recv()
                d_d(s_2, pO).start()
                for half in range(2):
                    d_g(s_2, par, 1, half).wait_send()
                for e in range(2):
                    d_r(s_2, par, e).wait_send()

            for half in range(2):
                d_g(s_2, par, 0, half).wait_send()

        for full, blocks in ((True, CHIPS), (False, CHIPS // 2)):
            @when(live_3, fag_3 if full else jnp.logical_not(fag_3))
            def _():
                d_d_all(s_3, blocks).wait_recv()
                d_d_all(s_3, blocks).wait_send()

        for s in range(STREAMS):
            @when(m3 == NS - STREAMS + s)
            def _():
                for w in out_copies(s):
                    w.start()

        r8 = lax.rem(mc, 8)
        rows8 = lax.broadcasted_iota(jnp.int32, (8, hd), 0)

        def half_cols(half, k):
            return pl.ds(pl.multiple_of(half * DH + k * hd, hd), hd)

        def decode_send():
            for slot_, half in ((E_OUT, 1 - c), (E_A, c)):
                for t in range(NT4):
                    acc = DP[:, half_cols(half, 4 * t)]
                    for q in range(1, 4):
                        acc = acc + pltpu.roll(DP[:, half_cols(half, 4 * t + q)], 2 * q, axis=0)
                    EX[slot_, t] = acc
            d_e(0).start()

        @when(jnp.logical_or(r8 == 5, jnp.logical_and(r8 == 0, mc > 0)))
        def _():
            d_e(0).wait_recv()
            d_e(0).wait_send()
            EX[E_A] = EX[E_A] + EX[E_IN0]
            d_e(1).start()

        @when(jnp.logical_or(r8 == 6, jnp.logical_and(r8 == 1, mc > 8)))
        def _():
            d_e(2).wait_recv()
            d_e(2).wait_send()
            EX[E_C] = EX[E_B] + EX[E_IN2]
            d_e(3).start()

        @when(jnp.logical_or(r8 == 7, jnp.logical_and(r8 == 2, mc > 8)))
        def _():
            d_e(3).wait_recv()
            d_e(3).wait_send()
            for slot_, half in ((E_C, c), (E_IN3, 1 - c)):
                for t in range(NT4):
                    block = EX[slot_, t]
                    for q in range(4):
                        part = block if q == 0 else pltpu.roll(block, 8 - 2 * q, axis=0)
                        cols = half_cols(half, 4 * t + q)
                        DY[:, cols] = DY[:, cols] + jnp.where(rows8 < 2, part, 0.0)
            lq = lax.div(mc, 8)

            @when(r8 == 7)
            def _():
                decode_norm(g2[pl.ds(lq, 1), :])

            @when(r8 == 2, mc < NS)
            def _():
                decode_norm(g1[pl.ds(jnp.minimum(lq, L - 1), 1), :])

        par_c = lax.rem(mc, 2)
        sc = lax.rem(mc, STREAMS)
        lq_c = jnp.minimum(lax.div(mc, 8), L - 1)
        attn_c = jnp.logical_and(live_c, r8 < 4)
        mlp_c = jnp.logical_and(live_c, r8 >= 4)

        for s in range(STREAMS):
            @when(mc == s)
            def _():
                for w in prompt_copies(s):
                    w.wait()

                def first_rows(i, _):
                    rows = pl.ds(pl.multiple_of(i * BR, BR), BR)
                    hn = normed(H[s, rows, :].astype(F32), g1[0:1, :])
                    H[s, rows, :] = hn.astype(BF16)
                    return 0

                XR[s] = H[s, rows_of(pX), :]
                lax.fori_loop(0, n_tp, first_rows, 0)

        NQKV = (G + 2) * hd

        def qkv_tiles(fn):
            c0 = 0
            while c0 < NQKV:
                c1 = min(c0 + 2 * hd, NQKV)
                fn(c0, c1)
                c0 = c1

        @when(attn_c)
        def _():
            @when(sc == 0)
            def _():
                for w in wa_copies(lq_c):
                    w.wait()

                @when(mc == 0)
                def _():
                    for s in range(1, STREAMS):
                        for w in prompt_copies(s):
                            w.start()
                    for w in wm_copies(0):
                        w.start()

                @when(mc > 0)
                def _():
                    for w in wf_copies(lq_c):
                        w.wait()

            @when(mc < 8)
            def _():
                def go(c0, c1):
                    QS[:, c0:c1] = jnp.dot(H[sc], WQ[:, c0:c1], preferred_element_type=F32).astype(BF16)

                qkv_tiles(go)

            @when(mc >= 8)
            def _():
                home = pl.ds(pl.multiple_of(hp * HS, HS), HS)

                def go(c0, c1):
                    for f, w in enumerate((WQ, WQF)):
                        QS[f * HS:(f + 1) * HS, c0:c1] = jnp.dot(
                            H[sc, home, :], w[:, c0:c1], preferred_element_type=F32).astype(BF16)

                qkv_tiles(go)

                @when(sc == STREAMS - 1)
                def _():
                    def dec(c0, c1):
                        QS[TS:TS + DEC, c0:c1] = jnp.dot(
                            H[STREAMS - 1, TS:TS + DEC, :], WQ[:, c0:c1], preferred_element_type=F32).astype(BF16)

                    qkv_tiles(dec)

            for f in range(2):
                for kv in range(2):
                    KV[f, kv, quarter(sc), :] = QS[f * HS:(f + 1) * HS, (G + kv) * hd:(G + kv + 1) * hd]

            @when(mc < 8)
            def _():
                for f in range(2):
                    d_kv(lq_c, f, f, sc, {'ho': up}).start()

            @when(mc >= 8)
            def _():
                d_kv(lq_c, 0, hp, sc, {'ho': up}).start()
                d_kv(lq_c, 1, hp, sc, {'ho': up, 'tp': V * CORES + c}).start()

            RT = tile_of(HS, 128)

            def attn_tile(i, _):
                g = lax.div(i, TS // RT)
                r = lax.rem(i, TS // RT)
                f = lax.div(r, HS // RT)
                rows = pl.ds(pl.multiple_of(r * RT, RT), RT)
                cols = pl.ds(pl.multiple_of(g * hd, hd), hd)
                q = QS[rows, cols]
                scores = lax.dot_general(q, KV[f, 0], (((1,), (1,)), ((), ())), preferred_element_type=F32) * scale
                qpos = sc * HS + lax.rem(r, HS // RT) * RT + lax.broadcasted_iota(jnp.int32, (RT, T), 0)
                kpos = lax.broadcasted_iota(jnp.int32, (RT, T), 1)
                scores = jnp.where(qpos >= kpos, scores, -1e30)
                e = jnp.exp(scores - jnp.max(scores, axis=-1, keepdims=True))
                p = (e / jnp.sum(e, axis=-1, keepdims=True)).astype(BF16)
                OS[rows, cols] = jnp.dot(p, KV[f, 1], preferred_element_type=F32).astype(BF16)
                return 0

            lax.fori_loop(0, G * (TS // RT), attn_tile, 0)

        UT = tile_of(F, 256)

        @when(mlp_c)
        def _():
            @when(sc == 0)
            def _():
                for w in wm_copies(lq_c):
                    w.wait()

            def gate_up(i, _):
                cols = pl.ds(pl.multiple_of(i * UT, UT), UT)
                gate = jnp.dot(H[sc], WG[:, cols], preferred_element_type=F32)
                up_ = jnp.dot(H[sc], WU[:, cols], preferred_element_type=F32)
                US[:, cols] = (gate * (1.0 / (1.0 + jnp.exp(-gate))) * up_).astype(BF16)
                return 0

            lax.fori_loop(0, F // UT, gate_up, 0)

        @when(live_n, frs_n, jnp.logical_not(heavy))
        def _():
            for e in range(2):
                d_a(par_n, e).wait_recv()
                PB[par_n, e, pN[1 - e], c] = PB[par_n, e, pN[1 - e], c] + AR[par_n, e]
            for e in range(2):
                d_c(par_n, s_n, 1 - e).start()

        @when(heavy)
        def _():
            for e in range(2):
                d_a(par_n, e, True).wait_recv()
                PB[par_n, e, pV, c] = PB[par_n, e, pV, c] + AR[par_n, e]
            d_c(par_n, s_n, 1).start()
            d_b(par_n, s_n, 1).start()

        NT = tile_of(DH, 512)

        def at_cols(t):
            return pl.ds(pl.multiple_of(t * NT, NT), NT)

        @when(attn_c, mc < 8)
        def _():
            for h in range(2):
                def out_tile(t, _):
                    cols = pl.ds(pl.multiple_of(h * DH + t * NT, NT), NT)
                    val = jnp.dot(OS[...], WO[:, cols], preferred_element_type=F32)
                    PB[par_c, h, :, :, :, at_cols(t)] = val.astype(BF16).reshape(CHIPS, CORES, BR, NT)
                    return 0

                lax.fori_loop(0, DH // NT, out_tile, 0)
                d_pr(par_c, h).start()

        @when(attn_c, mc >= 8)
        def _():
            for h in range(2):
                def out_tile(t, _):
                    cols = pl.ds(pl.multiple_of(h * DH + t * NT, NT), NT)
                    val = jnp.dot(OS[0:HS, :], WO[:, cols], preferred_element_type=F32)
                    val = val + jnp.dot(OS[HS:TS, :], WOF[:, cols], preferred_element_type=F32)
                    PB[par_c, h, pl.ds(hp * 2, 2), :, :, at_cols(t)] = val.astype(BF16).reshape(2, CORES, BR, NT)
                    return 0

                lax.fori_loop(0, DH // NT, out_tile, 0)
                d_pr_home(par_c, h).start()

        @when(mlp_c)
        def _():
            for h in range(2):
                def down_tile(t, _):
                    cols = pl.ds(pl.multiple_of(h * DH + t * NT, NT), NT)
                    val = jnp.dot(US[...], WD[:, cols], preferred_element_type=F32)
                    PB[par_c, h, :, :, :, at_cols(t)] = val[0:TS].astype(BF16).reshape(CHIPS, CORES, BR, NT)
                    DP[:, cols] = val[TS:TS + 8]
                    return 0

                lax.fori_loop(0, DH // NT, down_tile, 0)
                d_pr(par_c, h).start()

        @when(n < NS + 2)
        def _():
            for e in range(2):
                pl.semaphore_signal(s_sync.at[e], inc=1, device_id=to_near[e], device_id_type=MESH)

        @when(live_1, fag_1)
        def _():
            for e in range(2):
                d_g(s_1, par_1, e, e).wait_recv()
                d_r(s_1, par_1, e).start()

        @when(jnp.logical_or(r8 == 5, jnp.logical_and(r8 == 0, mc > 0)))
        def _():
            d_e(1).wait_recv()
            d_e(1).wait_send()
            EX[E_B] = EX[E_A] + EX[E_IN1]
            d_e(2).start()

        @when(live_c, r8 == 4)
        def _():
            for pr in range(2):
                d_kv_all(lq_c, pr, pr).wait_send()
            for pr in range(2):
                d_kv_all(lq_c, pr, pr).wait_recv()
            rows = lax.broadcasted_iota(jnp.int32, (DEC, hd), 0)
            outs = []
            for pr in range(2):
                @when(lq_c > 0)
                def _():
                    cache_copy(lq_c - 1, pr).wait()

                both = jnp.zeros((DEC, hd), F32)
                for kv in range(2):
                    new = QS[TS:TS + DEC, (G + kv) * hd:(G + kv + 1) * hd].astype(F32)
                    new = jnp.sum(jnp.where(rows == pr, new, 0.0), axis=0, keepdims=True)
                    KVR[lq_c, pr, kv, T:T + DEC, :] = jnp.where(rows == 0, new, 0.0).astype(BF16)
                    both = jnp.where(rows == kv, new, both)
                    Z32[pl.ds(kv, T, stride=2), :] = KVR[lq_c, pr, kv, 0:T, :].astype(F32)
                ZB[pr, 0:T] = Z32[...].astype(BF16).reshape(T, 2, hd)
                ZB[pr, T:T + DEC // 2] = both.astype(BF16).reshape(DEC // 2, 2, hd)
                cache_copy(lq_c, pr).start()
                q = jnp.concatenate([QS[TS:TS + DEC, g * hd:(g + 1) * hd] for g in range(G)], axis=0)
                scores = lax.dot_general(q, KVR[lq_c, pr, 0], (((1,), (1,)), ((), ())), preferred_element_type=F32) * scale
                kpos = lax.broadcasted_iota(jnp.int32, (G * DEC, T + PAD), 1)
                scores = jnp.where(kpos <= T, scores, -1e30)
                e = jnp.exp(scores - jnp.max(scores, axis=-1, keepdims=True))
                p = (e / jnp.sum(e, axis=-1, keepdims=True)).astype(BF16)
                outs.append(jnp.dot(p, KVR[lq_c, pr, 1], preferred_element_type=F32))
            picked = []
            for g in range(G):
                rest = jnp.where(rows == 1, outs[1][g * DEC:(g + 1) * DEC], 0.0)
                picked.append(jnp.where(rows == 0, outs[0][g * DEC:(g + 1) * DEC], rest).astype(BF16))
            od = jnp.concatenate(picked, axis=1)

            for t in range(D // NT):
                part = jnp.dot(od, WO[:, t * NT:(t + 1) * NT], preferred_element_type=F32)
                DP[:, t * NT:(t + 1) * NT] = part[0:8]
            decode_send()

            @when(lax.div(mc, 8) + 1 < L)
            def _():
                for w in wa_copies(lax.div(mc, 8) + 1):
                    w.start()

        @when(live_c, r8 == 7)
        def _():
            decode_send()

            @when(lax.div(mc, 8) + 1 < L)
            def _():
                for w in wm_copies(lax.div(mc, 8) + 1):
                    w.start()

        def by_parity(k, even, odd):
            if isinstance(k, int):
                (odd if k % 2 else even)()
            else:
                when(lax.rem(k, 2) == 0)(even)
                when(lax.rem(k, 2) == 1)(odd)

        def arrived(l, k, wide):
            opposite = lax.rem(j + 2, n_ho)
            d_on(l, k, wide, opposite, {'ho': up}).wait_recv()
            d_on(l, k, wide, opposite, {'ho': up}).wait_send()

        def pass_on(l, k, wide):
            d_up(l, k, wide, j).wait_recv()
            d_down(l, k, wide, j).wait_recv()
            by_parity(k, lambda: d_on(l, k, wide, down, {'ho': up}).start(),
                      lambda: d_on(l, k, wide, up, {'ho': down}).start())
            d_up(l, k, wide, j).wait_send()
            d_down(l, k, wide, j).wait_send()

        def spread(l, k, wide):
            d_x(l, k, wide).wait_recv()
            d_up(l, k, wide, j).start()
            d_down(l, k, wide, j).start()
            d_x(l, k, wide).wait_send()

        pieces(n - 3, arrived)
        pieces(n - 2, pass_on)
        pieces(n - 1, spread)

        @when(mc >= 7, r8 == 7, lax.div(mc, 8) + 1 < L)
        def _():
            for w in wf_copies(lax.div(mc, 8) + 1):
                w.start()

        return 0

    lax.fori_loop(0, NS + 4, slot, 0)

    fin_a[...] = DY[0:1, :]
    fin_b[...] = DY[1:2, :]
    for pr in range(2):
        cache_copy(L - 1, pr).wait()
    for s in range(STREAMS):
        for w in out_copies(s):
            w.wait()


def device_specs():
    row_axes = ('pairs', 'ho')
    in_specs = (P('pairs', None, None), P('pairs', None, None), P(row_axes, None), P(row_axes, None),
                P(None, None, 'tp', None, None), P(None, 'tp', None, None, None), P(None, None, 'tp'),
                P(None, None, 'tp'), P(None, 'tp', None), P(None, None), P(None, None))
    out_specs = (P(row_axes, None, None), P(row_axes, None, None), P(row_axes, None), P(row_axes, None),
                 P(row_axes, None, None, None, 'tp', None), P(row_axes, None, None, None, 'tp', None))
    return in_specs, out_specs


def solution(mesh):
    n_ho, n_tp = mesh.shape['ho'], mesh.shape['tp']
    in_specs, out_specs = device_specs()

    def per_device(prompt_a, prompt_b, first_a, first_b, w_qkv, w_out, w_gate, w_up, w_down, norm_attn, norm_mlp):
        L, D = w_qkv.shape[0], w_qkv.shape[1]
        G, hd = w_out.shape[2], w_out.shape[3]
        F = w_gate.shape[2]
        T = prompt_a.shape[1]
        TS, DH = T // 2, D // 2
        BR = TS // n_tp
        wq = jnp.transpose(w_qkv[:, :, 0], (0, 2, 1, 3))
        wo = w_out.reshape(L, G * hd, D)
        any_spec = pl.BlockSpec(memory_space=pl.ANY)
        hbm_spec = pl.BlockSpec(memory_space=pltpu.HBM)
        vmem_spec = pl.BlockSpec(memory_space=pltpu.VMEM)
        dma = pltpu.SemaphoreType.DMA
        flops = 2 * L * 2 * T * D * (wq.shape[1] * hd + G * hd + 3 * F)
        outs = pl.pallas_call(
            functools.partial(body, (n_ho, n_tp, L, T, D, G, hd, F)),
            name='serve',
            out_shape=(
                jax.ShapeDtypeStruct((T, D), BF16), jax.ShapeDtypeStruct((T, D), BF16),
                jax.ShapeDtypeStruct((1, D), F32), jax.ShapeDtypeStruct((1, D), F32),
                jax.ShapeDtypeStruct((L * (T + 1), 2, hd), BF16), jax.ShapeDtypeStruct((L * (T + 1), 2, hd), BF16),
                jax.ShapeDtypeStruct((L - 1, G + 2, D, hd), BF16), jax.ShapeDtypeStruct((L - 1, G * hd, D), BF16)),
            in_specs=[hbm_spec] * 11,
            out_specs=(any_spec, any_spec, vmem_spec, vmem_spec, any_spec, any_spec, hbm_spec, hbm_spec),
            scratch_shapes=[
                pltpu.VMEM((STREAMS, TS + DEC, D), BF16),
                pltpu.VMEM((2, 2, CHIPS, CORES, BR, DH), BF16),
                pltpu.VMEM((2, 2, CHIPS, BR, DH), BF16),
                pltpu.VMEM((2, 2, BR, DH), BF16),
                pltpu.VMEM((STREAMS, 2, 2, BR, DH), BF16),
                pltpu.VMEM((STREAMS, BR, D), BF16),
                pltpu.VMEM((TS + DEC, (G + 2) * hd), BF16),
                pltpu.VMEM((2, 2, T, hd), BF16),
                pltpu.VMEM((TS, G * hd), BF16),
                pltpu.VMEM((TS + DEC, F), BF16),
                pltpu.VMEM((L, 2, 2, T + PAD, hd), BF16),
                pltpu.VMEM((D, (G + 2) * hd), BF16),
                pltpu.VMEM((G * hd, D), BF16),
                pltpu.VMEM((D, (G + 2) * hd), BF16),
                pltpu.VMEM((G * hd, D), BF16),
                pltpu.VMEM((D, F), BF16),
                pltpu.VMEM((D, F), BF16),
                pltpu.VMEM((F, D), BF16),
                pltpu.VMEM((L, D), F32),
                pltpu.VMEM((L, D), F32),
                pltpu.VMEM((2, 1, D), BF16),
                pltpu.VMEM((8, D), F32),
                pltpu.VMEM((8, D), F32),
                pltpu.VMEM((8, DH // (4 * hd), 8, hd), F32),
                pltpu.VMEM((2 * T, hd), F32),
                pltpu.VMEM((2, T + 8, 2, hd), BF16),
                dma((2, 2)), dma((2, 2)),
                dma((2, 2)), dma((2, 2)),
                dma((STREAMS, 2)), dma((STREAMS, 2)),
                dma((STREAMS, 2)), dma((STREAMS, 2)),
                dma((2, 2, 2)), dma((2, 2, 2)),
                dma((2, 2)), dma((2, 2)),
                dma((STREAMS,)), dma((STREAMS,)),
                dma((2,)), dma((L, 2)),
                dma((G + 3,)), dma((G + 3,)), dma((3,)),
                dma((STREAMS, 2)), dma((STREAMS, 2)), dma((2,)),
                dma((4,)), dma((4,)), dma((4,)),
                dma((8,)), dma((8,)), dma((8,)), dma((8,)), dma((8,)), dma((8,)), dma((8,)), dma((8,)),
                pltpu.SemaphoreType.REGULAR((2,)),
            ],
            compiler_params=pltpu.CompilerParams(
                collective_id=0, has_side_effects=True, vmem_limit_bytes=54 * 1024 * 1024),
            cost_estimate=pl.CostEstimate(flops=flops, bytes_accessed=2 * L * D * (5 * hd + G * hd + 3 * F), transcendentals=0),
        )(prompt_a, prompt_b, first_a, first_b, wq, wo, w_gate, w_up, w_down, norm_attn, norm_mlp)
        out_a, out_b, fin_a, fin_b, cache_a, cache_b = outs[:6]

        def cache(rows):
            return jnp.transpose(rows.reshape(L, T + 1, 2, hd), (0, 2, 1, 3))[None, :, :, :, None, :]

        return (out_a[None], out_b[None], fin_a, fin_b, cache(cache_a), cache(cache_b))

    return jax.shard_map(per_device, mesh=mesh, in_specs=in_specs, out_specs=out_specs, check_vma=False)
```

time: 645 us -> 640 us (level)
  no operation moved by 1% of the time
where the time goes in v3:
time: 640 us
  Pallas kernels  628 us (98%)
  local copies, waits for them, and re-layouts  11.2 us (2%)
    pallas_call x1, Pallas kernels, per_device(): pl.pallas_call(functools.partial(body, (n_ho, n_tp, L, T, D, G, hd, F)),...  628 us

profile of v3, /device:TPU:97, one launch (start us, length us, event | category | flops | bytes accessed | tf_op | source)
XLA Modules:
  0.0 639.8 jit_solution(10592005478334456271)
XLA Ops:
  0.6 628.0 %serve.1 = (bf16[512,3072]{1,0:T(8,128)(2,1)}, bf16[512,3072]{1,0:T(8,128)(2,1)}, f32[1,3072]{1,0:T(1,128)}, f32[1,3072]{1,0:T(1,128)}, bf16[3078,2,128]{2,1,0:T...) custom-call(bf16[4,512,3072]{2,1,0:T(8,128)(2,1)} %pa.1, ...), custom_call_target="tpu_custom_call" | custom-call | flops 154618822656 | bytes 150994944 | tf_op jit(solution)/shard_map/serve/pallas_call | solution.py:788
  628.6 0.0 copy-start.3
  628.6 0.0 copy-start.2
  628.6 0.0 copy-start.1
  628.6 0.0 copy-start
  628.7 3.9 copy.23
  632.6 3.8 copy.24
  636.3 0.0 copy-done.3
  636.3 0.6 copy.25
  636.9 0.0 copy-done.2
  636.9 0.6 copy.26
  637.5 0.0 copy-done.1
  637.5 1.1 copy.27
  638.7 0.0 copy-done
  638.7 1.1 copy.28
Async XLA Ops:
  628.6 7.7 %copy-start.3 = (f32[1,3072]{1,0:T(1,128)S(1)}, f32[1,3072]{1,0:T(1,128)}, u32[]{:S(2)}) copy-start(f32[1,3072]{1,0:T(1,128)} %get-tuple-element.26) | copy-start | bytes 36868
  628.6 8.3 %copy-start.2 = (f32[1,3072]{1,0:T(1,128)S(1)}, f32[1,3072]{1,0:T(1,128)}, u32[]{:S(2)}) copy-start(f32[1,3072]{1,0:T(1,128)} %get-tuple-element.27) | copy-start | bytes 36868
  628.6 8.9 %copy-start.1 = (bf16[3078,2,128]{2,1,0:T(2,128)(2,1)S(1)}, bf16[3078,2,128]{2,1,0:T(2,128)(2,1)}, u32[]{:S(2)}) copy-start(bf16[3078,2,128]{2,1,0:T(2,128)(2,1)} %get-tuple-element.16) | copy-start | bytes 4727812
  628.6 10.0 %copy-start = (bf16[3078,2,128]{2,1,0:T(2,128)(2,1)S(1)}, bf16[3078,2,128]{2,1,0:T(2,128)(2,1)}, u32[]{:S(2)}) copy-start(bf16[3078,2,128]{2,1,0:T(2,128)(2,1)} %get-tuple-element.17) | copy-start | bytes 4727812

commit v4 on v3

--- a/solution.py
+++ b/solution.py
@@ -12,6 +12,7 @@
 BF16 = jnp.bfloat16
 CORES = 2
 CHIPS = 4
+BOTH = range(2)
 STREAMS = 4
 DEC = 16
 PAD = 128
@@ -24,10 +25,10 @@
     return tile
 
 
-def body(cfg, pa, pb, fa, fb, wq, wo, wg, wu, wd, g1h, g2h, oa, ob, fin_a, fin_b, ca, cb, fq, fo,
-         H, PB, PR, AR, BC, XR, QS, KV, OS, US, KVR, WQ, WO, WQF, WOF, WG, WU, WD, g1, g2, FT, DY, DP, EX, Z32, ZB,
+def body(cfg, pa, pb, fa, fb, wq, wo, wg, wu, wd, g1h, g2h, oa, ob, fin_a, fin_b, ca, cb,
+         H, PB, PR, AR, BC, XR, QS, KV, OS, US, KVR, WQ, WO, WQF, WOF, XSQ, XSO, WG, WU, WD, g1, g2, FT, DY, DP, EX, Z32, ZB,
          s_prs, s_prr, s_as, s_ar, s_bs, s_br, s_cs, s_cr, s_gs, s_gr, s_rs, s_rr, s_ds, s_dr,
-         s_kvs, s_kvr, s_wa, s_wf, s_wm, s_in, s_out, s_ko, s_es, s_er, s_sm,
+         s_kvs, s_kvr, s_wa, s_ps, s_wm, s_in, s_out, s_ko, s_es, s_er, s_sm,
          s_xs, s_xr, s_us, s_ur, s_ls, s_lr, s_ys, s_yr, s_sync):
     n_ho, n_tp, L, T, D, G, hd, F = cfg
     TS = T // 2
@@ -120,36 +121,40 @@
     def cache_copy(l, pr):
         return lc(ZB.at[pr, pl.ds(0, T + 1)], (cb if pr else ca).at[pl.ds(l * (T + 1), T + 1)], s_ko.at[pr])
 
-    def piece(refs, l, k, wide, r):
+    def piece(l, k, wide, r):
+        par = lax.rem(l, 2)
         if wide:
-            return refs[0].at[l, k, pl.ds(pl.multiple_of(r * DQ, DQ), DQ), :]
-        return refs[1].at[l, pl.ds(pl.multiple_of(r * OQ + (k - (G + 2)) * OC, OC), OC), :]
+            return WQF.at[par, pl.ds(pl.multiple_of(r * DQ, DQ), DQ), pl.ds(pl.multiple_of(k * hd, hd), hd)]
+        return WOF.at[par, pl.ds(pl.multiple_of(r * OQ + (k - (G + 2)) * OC, OC), OC), :]
+
+    def fetched(k, wide):
+        return XSQ.at[k] if wide else XSO.at[k - (G + 2)]
+
+    def d_fetch(l, k, wide):
+        if wide:
+            src = wq.at[l, k, pl.ds(pl.multiple_of(j * DQ, DQ), DQ), :]
+        else:
+            src = wo.at[l, pl.ds(pl.multiple_of(j * OQ + (k - (G + 2)) * OC, OC), OC), :]
+        return lc(src, fetched(k, wide), s_ps.at[k])
 
     def d_x(l, k, wide):
-        return rc(piece((wq, wo), l, k, wide, j), piece((fq, fo), l - 1, k, wide, j), s_xs.at[k], s_xr.at[k], to_near[1])
+        return rc(fetched(k, wide), piece(l, k, wide, j), s_xs.at[k], s_xr.at[k], to_near[1])
 
     def d_up(l, k, wide, r):
-        ref = piece((fq, fo), l - 1, k, wide, r)
-        return rc(ref, ref, s_us.at[k], s_ur.at[k], {'ho': up})
+        return rc(piece(l, k, wide, r), piece(l, k, wide, r), s_us.at[k], s_ur.at[k], {'ho': up})
 
     def d_down(l, k, wide, r):
-        ref = piece((fq, fo), l - 1, k, wide, r)
-        return rc(ref, ref, s_ls.at[k], s_lr.at[k], {'ho': down})
+        return rc(piece(l, k, wide, r), piece(l, k, wide, r), s_ls.at[k], s_lr.at[k], {'ho': down})
 
     def d_on(l, k, wide, r, dev):
-        ref = piece((fq, fo), l - 1, k, wide, r)
-        return rc(ref, ref, s_ys.at[k], s_yr.at[k], dev)
+        return rc(piece(l, k, wide, r), piece(l, k, wide, r), s_ys.at[k], s_yr.at[k], dev)
 
     def wa_copies(l):
         out = [lc(wq.at[l, i], WQ.at[:, pl.ds(i * hd, hd)], s_wa.at[i]) for i in range(G + 2)]
         return out + [lc(wo.at[l], WO, s_wa.at[G + 2])]
 
-    def wf_copies(l):
-        out = [lc(fq.at[l - 1, i], WQF.at[:, pl.ds(i * hd, hd)], s_wf.at[i]) for i in range(G + 2)]
-        return out + [lc(fo.at[l - 1], WOF, s_wf.at[G + 2])]
-
     def wm_copies(l):
-        return [lc(wg.at[l], WG, s_wm.at[0]), lc(wu.at[l], WU, s_wm.at[1]), lc(wd.at[l], WD, s_wm.at[2])]
+        return [lc(src.at[l], dst, s_wm.at[i]) for i, (src, dst) in enumerate(((wg, WG), (wu, WU), (wd, WD)))]
 
     def prompt_copies(s):
         return [lc(p.at[j, pl.ds(s * HS, HS)], H.at[s, pl.ds(i * HS, HS)], s_in.at[s, i]) for i, p in enumerate((pa, pb))]
@@ -157,7 +162,8 @@
     def out_copies(s):
         return [lc(H.at[s, pl.ds(i * HS, HS)], o.at[pl.ds(s * HS, HS)], s_out.at[s, i]) for i, o in enumerate((oa, ob))]
 
-    small = [lc(g1h, g1, s_sm.at[0]), lc(g2h, g2, s_sm.at[1]), lc(fa, FT.at[0], s_sm.at[2]), lc(fb, FT.at[1], s_sm.at[3])]
+    small = [lc(src, dst, s_sm.at[i])
+             for i, (src, dst) in enumerate(((g1h, g1), (g2h, g2), (fa, FT.at[0]), (fb, FT.at[1])))]
 
     barrier = pltpu.get_barrier_semaphore()
     met = [to_partner, to_near[0], to_near[1], {'ho': up}, {'ho': down},
@@ -165,15 +171,15 @@
     for dev in met:
         pl.semaphore_signal(barrier, inc=1, device_id=dev, device_id_type=MESH)
 
-    for w in prompt_copies(0) + small + wa_copies(0):
+    for w in prompt_copies(0) + small + [d_fetch(1, k, True) for k in range(3)] + wa_copies(0):
         w.start()
     KV[...] = jnp.zeros(KV.shape, BF16)
     for s in range(STREAMS):
         H[s, TS:TS + DEC, :] = jnp.zeros((DEC, D), BF16)
 
     def zero_kvr(l, _):
-        for pr in range(2):
-            for kv in range(2):
+        for pr in BOTH:
+            for kv in BOTH:
                 KVR[l, pr, kv, T:T + PAD, :] = jnp.zeros((PAD, hd), BF16)
         return 0
 
@@ -190,8 +196,8 @@
     for w in small:
         w.wait()
     DY[...] = jnp.zeros(DY.shape, F32)
-    DY[0:1, :] = FT[0].astype(F32)
-    DY[1:2, :] = FT[1].astype(F32)
+    for i in BOTH:
+        DY[i:i + 1, :] = FT[i].astype(F32)
     decode_norm(g1[0:1, :])
     pl.semaphore_wait(barrier, len(met))
 
@@ -226,45 +232,45 @@
 
         @when(live_n, frs_n)
         def _():
-            for h in range(2):
+            for h in BOTH:
                 d_pr(par_n, h).wait_recv()
-            for e in range(2):
+            for e in BOTH:
                 add(e, pO)
 
             @when(jnp.logical_not(heavy))
             def _():
-                for e in range(2):
+                for e in BOTH:
                     d_a(par_n, e).start()
-                for e in range(2):
+                for e in BOTH:
                     add(e, pN[e])
-                for e in range(2):
+                for e in BOTH:
                     d_b(par_n, s_n, e).start()
-                for e in range(2):
+                for e in BOTH:
                     add(1 - e, pN[e])
 
             @when(heavy)
             def _():
-                for e in range(2):
+                for e in BOTH:
                     d_a(par_n, e, True).start()
-                for e in range(2):
+                for e in BOTH:
                     add(e, pQ)
                 d_b(par_n, s_n, 0).start()
                 d_c(par_n, s_n, 0).start()
-                for e in range(2):
+                for e in BOTH:
                     add(e, pV)
 
-            for e in range(2):
+            for e in BOTH:
                 add(e, pX)
 
         @when(live_n, jnp.logical_not(frs_n))
         def _():
-            for h in range(2):
+            for h in BOTH:
                 d_pr_home(par_n, h).wait_recv()
-            for h in range(2):
+            for h in BOTH:
                 add(h, pQ)
             d_b(par_n, s_n, 0).start()
             d_c(par_n, s_n, 0).start()
-            for h in range(2):
+            for h in BOTH:
                 add(h, pX)
 
         def pieces(t, fn):
@@ -288,11 +294,41 @@
             def _():
                 fn(lax.div(t, 8) + 2, r - 5, True)
 
-        pieces(n, lambda l, k, wide: d_x(l, k, wide).start())
+        def by_parity(k, even, odd):
+            if isinstance(k, int):
+                (odd if k % 2 else even)()
+            else:
+                when(lax.rem(k, 2) == 0)(even)
+                when(lax.rem(k, 2) == 1)(odd)
+
+        def arrived(l, k, wide):
+            opposite = lax.rem(j + 2, n_ho)
+            d_on(l, k, wide, opposite, {'ho': up}).wait_recv()
+            d_on(l, k, wide, opposite, {'ho': up}).wait_send()
+
+        def pass_on(l, k, wide):
+            d_up(l, k, wide, j).wait_recv()
+            d_down(l, k, wide, j).wait_recv()
+            by_parity(k, lambda: d_on(l, k, wide, down, {'ho': up}).start(),
+                      lambda: d_on(l, k, wide, up, {'ho': down}).start())
+            d_up(l, k, wide, j).wait_send()
+            d_down(l, k, wide, j).wait_send()
+
+        def spread(l, k, wide):
+            d_x(l, k, wide).wait_recv()
+            d_up(l, k, wide, j).start()
+            d_down(l, k, wide, j).start()
+            d_x(l, k, wide).wait_send()
+
+        def send_over(l, k, wide):
+            d_fetch(l, k, wide).wait()
+            d_x(l, k, wide).start()
+
+        pieces(n, send_over)
 
         @when(n >= 0)
         def _():
-            for e in range(2):
+            for e in BOTH:
                 pl.semaphore_wait(s_sync.at[e], 1)
 
         @when(live_1)
@@ -310,7 +346,7 @@
 
             x_new = []
             ms = jnp.zeros((BR, 1), F32)
-            for h in range(2):
+            for h in BOTH:
                 second = jnp.where(frs_1, BC[s_1, 1, h].astype(F32), 0.0)
                 total = PB[par_1, h, pX, c].astype(F32) + (BC[s_1, 0, h].astype(F32) + second)
                 cols = slice(h * DH, (h + 1) * DH)
@@ -322,7 +358,7 @@
                 x_new.append(x)
             inv = lax.rsqrt(ms * (1.0 / D) + 1e-5)
             nl = jnp.minimum(l + 1, L - 1)
-            for h in range(2):
+            for h in BOTH:
                 cols = slice(h * DH, (h + 1) * DH)
                 gain = jnp.where(is_attn, g2[pl.ds(l, 1), cols], g1[pl.ds(nl, 1), cols])
                 hn = x_new[h] * inv * gain
@@ -349,16 +385,16 @@
 
             @when(frs_1)
             def _():
-                for h in range(2):
+                for h in BOTH:
                     d_pr(par_1, h).wait_send()
-                for e in range(2):
+                for e in BOTH:
                     d_a(par_1, e).wait_send()
                 d_b(par_1, s_1, 1).wait_send()
                 d_c(par_1, s_1, 1).wait_send()
 
             @when(jnp.logical_not(frs_1))
             def _():
-                for h in range(2):
+                for h in BOTH:
                     d_pr_home(par_1, h).wait_send()
 
         @when(live_2)
@@ -376,15 +412,15 @@
             def _():
                 d_g(s_2, par, 1, 0).wait_recv()
                 d_d(s_2, pV).start()
-                for e in range(2):
+                for e in BOTH:
                     d_r(s_2, par, e).wait_recv()
                 d_d(s_2, pO).start()
-                for half in range(2):
+                for half in BOTH:
                     d_g(s_2, par, 1, half).wait_send()
-                for e in range(2):
+                for e in BOTH:
                     d_r(s_2, par, e).wait_send()
 
-            for half in range(2):
+            for half in BOTH:
                 d_g(s_2, par, 0, half).wait_send()
 
         for full, blocks in ((True, CHIPS), (False, CHIPS // 2)):
@@ -398,6 +434,9 @@
             def _():
                 for w in out_copies(s):
                     w.start()
+
+        pieces(n - 4, arrived)
+        pieces(n - 1, spread)
 
         r8 = lax.rem(mc, 8)
         rows8 = lax.broadcasted_iota(jnp.int32, (8, hd), 0)
@@ -494,11 +533,6 @@
                     for w in wm_copies(0):
                         w.start()
 
-                @when(mc > 0)
-                def _():
-                    for w in wf_copies(lq_c):
-                        w.wait()
-
             @when(mc < 8)
             def _():
                 def go(c0, c1):
@@ -509,9 +543,10 @@
             @when(mc >= 8)
             def _():
                 home = pl.ds(pl.multiple_of(hp * HS, HS), HS)
+                lpar = lax.rem(lq_c, 2)
 
                 def go(c0, c1):
-                    for f, w in enumerate((WQ, WQF)):
+                    for f, w in enumerate((WQ, WQF.at[lpar])):
                         QS[f * HS:(f + 1) * HS, c0:c1] = jnp.dot(
                             H[sc, home, :], w[:, c0:c1], preferred_element_type=F32).astype(BF16)
 
@@ -525,13 +560,13 @@
 
                     qkv_tiles(dec)
 
-            for f in range(2):
-                for kv in range(2):
+            for f in BOTH:
+                for kv in BOTH:
                     KV[f, kv, quarter(sc), :] = QS[f * HS:(f + 1) * HS, (G + kv) * hd:(G + kv + 1) * hd]
 
             @when(mc < 8)
             def _():
-                for f in range(2):
+                for f in BOTH:
                     d_kv(lq_c, f, f, sc, {'ho': up}).start()
 
             @when(mc >= 8)
@@ -579,15 +614,15 @@
 
         @when(live_n, frs_n, jnp.logical_not(heavy))
         def _():
-            for e in range(2):
+            for e in BOTH:
                 d_a(par_n, e).wait_recv()
                 PB[par_n, e, pN[1 - e], c] = PB[par_n, e, pN[1 - e], c] + AR[par_n, e]
-            for e in range(2):
+            for e in BOTH:
                 d_c(par_n, s_n, 1 - e).start()
 
         @when(heavy)
         def _():
-            for e in range(2):
+            for e in BOTH:
                 d_a(par_n, e, True).wait_recv()
                 PB[par_n, e, pV, c] = PB[par_n, e, pV, c] + AR[par_n, e]
             d_c(par_n, s_n, 1).start()
@@ -600,7 +635,7 @@
 
         @when(attn_c, mc < 8)
         def _():
-            for h in range(2):
+            for h in BOTH:
                 def out_tile(t, _):
                     cols = pl.ds(pl.multiple_of(h * DH + t * NT, NT), NT)
                     val = jnp.dot(OS[...], WO[:, cols], preferred_element_type=F32)
@@ -612,11 +647,11 @@
 
         @when(attn_c, mc >= 8)
         def _():
-            for h in range(2):
+            for h in BOTH:
                 def out_tile(t, _):
                     cols = pl.ds(pl.multiple_of(h * DH + t * NT, NT), NT)
                     val = jnp.dot(OS[0:HS, :], WO[:, cols], preferred_element_type=F32)
-                    val = val + jnp.dot(OS[HS:TS, :], WOF[:, cols], preferred_element_type=F32)
+                    val = val + jnp.dot(OS[HS:TS, :], WOF[lax.rem(lq_c, 2), :, cols], preferred_element_type=F32)
                     PB[par_c, h, pl.ds(hp * 2, 2), :, :, at_cols(t)] = val.astype(BF16).reshape(2, CORES, BR, NT)
                     return 0
 
@@ -625,7 +660,7 @@
 
         @when(mlp_c)
         def _():
-            for h in range(2):
+            for h in BOTH:
                 def down_tile(t, _):
                     cols = pl.ds(pl.multiple_of(h * DH + t * NT, NT), NT)
                     val = jnp.dot(US[...], WD[:, cols], preferred_element_type=F32)
@@ -638,12 +673,12 @@
 
         @when(n < NS + 2)
         def _():
-            for e in range(2):
+            for e in BOTH:
                 pl.semaphore_signal(s_sync.at[e], inc=1, device_id=to_near[e], device_id_type=MESH)
 
         @when(live_1, fag_1)
         def _():
-            for e in range(2):
+            for e in BOTH:
                 d_g(s_1, par_1, e, e).wait_recv()
                 d_r(s_1, par_1, e).start()
 
@@ -656,19 +691,19 @@
 
         @when(live_c, r8 == 4)
         def _():
-            for pr in range(2):
+            for pr in BOTH:
                 d_kv_all(lq_c, pr, pr).wait_send()
-            for pr in range(2):
+            for pr in BOTH:
                 d_kv_all(lq_c, pr, pr).wait_recv()
             rows = lax.broadcasted_iota(jnp.int32, (DEC, hd), 0)
             outs = []
-            for pr in range(2):
+            for pr in BOTH:
                 @when(lq_c > 0)
                 def _():
                     cache_copy(lq_c - 1, pr).wait()
 
                 both = jnp.zeros((DEC, hd), F32)
-                for kv in range(2):
+                for kv in BOTH:
                     new = QS[TS:TS + DEC, (G + kv) * hd:(G + kv + 1) * hd].astype(F32)
                     new = jnp.sum(jnp.where(rows == pr, new, 0.0), axis=0, keepdims=True)
                     KVR[lq_c, pr, kv, T:T + DEC, :] = jnp.where(rows == 0, new, 0.0).astype(BF16)
@@ -709,48 +744,24 @@
                 for w in wm_copies(lax.div(mc, 8) + 1):
                     w.start()
 
-        def by_parity(k, even, odd):
-            if isinstance(k, int):
-                (odd if k % 2 else even)()
-            else:
-                when(lax.rem(k, 2) == 0)(even)
-                when(lax.rem(k, 2) == 1)(odd)
-
-        def arrived(l, k, wide):
-            opposite = lax.rem(j + 2, n_ho)
-            d_on(l, k, wide, opposite, {'ho': up}).wait_recv()
-            d_on(l, k, wide, opposite, {'ho': up}).wait_send()
-
-        def pass_on(l, k, wide):
-            d_up(l, k, wide, j).wait_recv()
-            d_down(l, k, wide, j).wait_recv()
-            by_parity(k, lambda: d_on(l, k, wide, down, {'ho': up}).start(),
-                      lambda: d_on(l, k, wide, up, {'ho': down}).start())
-            d_up(l, k, wide, j).wait_send()
-            d_down(l, k, wide, j).wait_send()
-
-        def spread(l, k, wide):
-            d_x(l, k, wide).wait_recv()
-            d_up(l, k, wide, j).start()
-            d_down(l, k, wide, j).start()
-            d_x(l, k, wide).wait_send()
-
-        pieces(n - 3, arrived)
         pieces(n - 2, pass_on)
-        pieces(n - 1, spread)
-
-        @when(mc >= 7, r8 == 7, lax.div(mc, 8) + 1 < L)
-        def _():
-            for w in wf_copies(lax.div(mc, 8) + 1):
-                w.start()
+
+        @when(n >= 0)
+        def _():
+            pieces(n + 1, lambda l, k, wide: d_fetch(l, k, wide).start())
+
+        @when(n == -1)
+        def _():
+            for k in (3, 4):
+                d_fetch(1, k, True).start()
 
         return 0
 
     lax.fori_loop(0, NS + 4, slot, 0)
 
-    fin_a[...] = DY[0:1, :]
-    fin_b[...] = DY[1:2, :]
-    for pr in range(2):
+    for i, ref in enumerate((fin_a, fin_b)):
+        ref[...] = DY[i:i + 1, :]
+    for pr in BOTH:
         cache_copy(L - 1, pr).wait()
     for s in range(STREAMS):
         for w in out_copies(s):
@@ -758,12 +769,10 @@
 
 
 def device_specs():
-    row_axes = ('pairs', 'ho')
-    in_specs = (P('pairs', None, None), P('pairs', None, None), P(row_axes, None), P(row_axes, None),
-                P(None, None, 'tp', None, None), P(None, 'tp', None, None, None), P(None, None, 'tp'),
-                P(None, None, 'tp'), P(None, 'tp', None), P(None, None), P(None, None))
-    out_specs = (P(row_axes, None, None), P(row_axes, None, None), P(row_axes, None), P(row_axes, None),
-                 P(row_axes, None, None, None, 'tp', None), P(row_axes, None, None, None, 'tp', None))
+    row, whole, last = P(('pairs', 'ho')), P(), P(None, None, 'tp')
+    in_specs = (P('pairs'), P('pairs'), row, row, last, P(None, 'tp'), last, last, P(None, 'tp'), whole, whole)
+    cache = P(('pairs', 'ho'), None, None, None, 'tp')
+    out_specs = (row, row, row, row, cache, cache)
     return in_specs, out_specs
 
 
@@ -778,23 +787,24 @@
         T = prompt_a.shape[1]
         TS, DH = T // 2, D // 2
         BR = TS // n_tp
-        wq = jnp.transpose(w_qkv[:, :, 0], (0, 2, 1, 3))
+        wq = jnp.swapaxes(w_qkv[:, :, 0], 1, 2)
         wo = w_out.reshape(L, G * hd, D)
         any_spec = pl.BlockSpec(memory_space=pl.ANY)
         hbm_spec = pl.BlockSpec(memory_space=pltpu.HBM)
         vmem_spec = pl.BlockSpec(memory_space=pltpu.VMEM)
         dma = pltpu.SemaphoreType.DMA
+        two, four, eight = (2, 2), (STREAMS,), (8,)
+        by_stream = four + two[:1]
         flops = 2 * L * 2 * T * D * (wq.shape[1] * hd + G * hd + 3 * F)
         outs = pl.pallas_call(
             functools.partial(body, (n_ho, n_tp, L, T, D, G, hd, F)),
             name='serve',
             out_shape=(
-                jax.ShapeDtypeStruct((T, D), BF16), jax.ShapeDtypeStruct((T, D), BF16),
+                jax.ShapeDtypeStruct((T + DEC, D), BF16), jax.ShapeDtypeStruct((T + DEC, D), BF16),
                 jax.ShapeDtypeStruct((1, D), F32), jax.ShapeDtypeStruct((1, D), F32),
-                jax.ShapeDtypeStruct((L * (T + 1), 2, hd), BF16), jax.ShapeDtypeStruct((L * (T + 1), 2, hd), BF16),
-                jax.ShapeDtypeStruct((L - 1, G + 2, D, hd), BF16), jax.ShapeDtypeStruct((L - 1, G * hd, D), BF16)),
+                jax.ShapeDtypeStruct((L * (T + 1), 2, hd), BF16), jax.ShapeDtypeStruct((L * (T + 1), 2, hd), BF16)),
             in_specs=[hbm_spec] * 11,
-            out_specs=(any_spec, any_spec, vmem_spec, vmem_spec, any_spec, any_spec, hbm_spec, hbm_spec),
+            out_specs=(any_spec, any_spec, vmem_spec, vmem_spec, any_spec, any_spec),
             scratch_shapes=[
                 pltpu.VMEM((STREAMS, TS + DEC, D), BF16),
                 pltpu.VMEM((2, 2, CHIPS, CORES, BR, DH), BF16),
@@ -809,8 +819,10 @@
                 pltpu.VMEM((L, 2, 2, T + PAD, hd), BF16),
                 pltpu.VMEM((D, (G + 2) * hd), BF16),
                 pltpu.VMEM((G * hd, D), BF16),
-                pltpu.VMEM((D, (G + 2) * hd), BF16),
-                pltpu.VMEM((G * hd, D), BF16),
+                pltpu.VMEM((2, D, (G + 2) * hd), BF16),
+                pltpu.VMEM((2, G * hd, D), BF16),
+                pltpu.VMEM((G + 2, D // n_ho, hd), BF16),
+                pltpu.VMEM((3, G * hd // n_ho // 3, D), BF16),
                 pltpu.VMEM((D, F), BF16),
                 pltpu.VMEM((D, F), BF16),
                 pltpu.VMEM((F, D), BF16),
@@ -822,29 +834,26 @@
                 pltpu.VMEM((8, DH // (4 * hd), 8, hd), F32),
                 pltpu.VMEM((2 * T, hd), F32),
                 pltpu.VMEM((2, T + 8, 2, hd), BF16),
-                dma((2, 2)), dma((2, 2)),
-                dma((2, 2)), dma((2, 2)),
-                dma((STREAMS, 2)), dma((STREAMS, 2)),
-                dma((STREAMS, 2)), dma((STREAMS, 2)),
-                dma((2, 2, 2)), dma((2, 2, 2)),
-                dma((2, 2)), dma((2, 2)),
-                dma((STREAMS,)), dma((STREAMS,)),
-                dma((2,)), dma((L, 2)),
-                dma((G + 3,)), dma((G + 3,)), dma((3,)),
-                dma((STREAMS, 2)), dma((STREAMS, 2)), dma((2,)),
-                dma((4,)), dma((4,)), dma((4,)),
-                dma((8,)), dma((8,)), dma((8,)), dma((8,)), dma((8,)), dma((8,)), dma((8,)), dma((8,)),
+                *map(dma, (two, two, two, two)),
+                *map(dma, (by_stream, by_stream, by_stream, by_stream)),
+                *map(dma, (two + two[:1], two + two[:1], two, two)),
+                *map(dma, (four, four)),
+                *map(dma, (two[:1], (L,) + two[:1])),
+                *map(dma, ((G + 3,), eight, (3,))),
+                *map(dma, (by_stream, by_stream, two[:1])),
+                *map(dma, (four, four, four)),
+                *map(dma, (eight,) * 8),
                 pltpu.SemaphoreType.REGULAR((2,)),
             ],
             compiler_params=pltpu.CompilerParams(
-                collective_id=0, has_side_effects=True, vmem_limit_bytes=54 * 1024 * 1024),
-            cost_estimate=pl.CostEstimate(flops=flops, bytes_accessed=2 * L * D * (5 * hd + G * hd + 3 * F), transcendentals=0),
+                collective_id=0, has_side_effects=True, vmem_limit_bytes=60 << 20),
+            cost_estimate=pl.CostEstimate(flops=flops, bytes_accessed=flops // T, transcendentals=0),
         )(prompt_a, prompt_b, first_a, first_b, wq, wo, w_gate, w_up, w_down, norm_attn, norm_mlp)
-        out_a, out_b, fin_a, fin_b, cache_a, cache_b = outs[:6]
+        out_a, out_b, fin_a, fin_b, cache_a, cache_b = outs
 
         def cache(rows):
-            return jnp.transpose(rows.reshape(L, T + 1, 2, hd), (0, 2, 1, 3))[None, :, :, :, None, :]
-
-        return (out_a[None], out_b[None], fin_a, fin_b, cache(cache_a), cache(cache_b))
+            return jnp.swapaxes(rows.reshape(L, T + 1, 2, hd), 1, 2)[None, :, :, :, None]
+
+        return (out_a[None, :T], out_b[None, :T], fin_a, fin_b, cache(cache_a), cache(cache_b))
 
     return jax.shard_map(per_device, mesh=mesh, in_specs=in_specs, out_specs=out_specs, check_vma=False)

time: 640 us -> 626 us (0.978)
  Pallas kernels: 628 us -> 615 us
    pallas_call x1, Pallas kernels: 628 us -> 615 us  [per_device(): pl.pallas_call(functools.partial(body, (n_ho, n_tp, L, T, D, G, hd, F)),...]
    unnamed x14 -> x12, local copies, waits for them, and re-layouts: 11.2 us -> 3.5 us
where the time goes in v4:
time: 626 us; the launch traced here: 625 us
  Pallas kernels  615 us (98%)
  local copies, waits for them, and re-layouts  9.6 us (2%)
    pallas_call x1, Pallas kernels, per_device(): pl.pallas_call(functools.partial(body, (n_ho, n_tp, L, T, D, G, hd, F)),...  615 us

profile of v4, /device:TPU:97, one launch (start us, length us, event | category | flops | bytes accessed | tf_op | source)
XLA Modules:
  0.0 624.9 jit_solution(17230222044973219369)
XLA Ops:
  0.6 614.7 %serve.1 = (bf16[528,3072]{1,0:T(8,128)(2,1)}, bf16[528,3072]{1,0:T(8,128)(2,1)}, f32[1,3072]{1,0:T(1,128)}, f32[1,3072]{1,0:T(1,128)}, bf16[3078,2,128]{2,1,0:T(2,128)(2,1)}, /*index=5*/bf16[3078,2,128]{2,1,0:T(2,128)(2,1)}) custom-call(bf16[4,512,3072]{2,1,0:T(8,128)(2,1)} %pa.1, bf16[4,512,3072]{2,1,0:T(8,128)(2,1)} %pb.1, bf16[1,3072]{1,0:T(2,128)(2,1)} %fa.1, ...), custom_call_target="tpu_custom_call" | custom-call | flops 154618822656 | bytes 301989888 | tf_op jit(solution)/shard_map/serve/pallas_call | solution.py:799
  615.3 0.0 copy-start.3
  615.3 0.0 copy-start.2
  615.3 0.0 copy-start.1
  615.3 6.1 slice_bitcast_fusion
  621.4 0.0 copy-start
  621.4 0.0 copy-done.3
  621.5 0.6 copy.21
  622.1 0.0 copy-done.2
  622.1 0.6 copy.22
  622.7 0.0 copy-done.1
  622.7 1.1 copy.23
  623.8 0.0 copy-done
  623.8 1.1 copy.24
Async XLA Ops:
  615.3 6.1 copy-start.3
  615.3 6.7 %copy-start.2 = (f32[1,3072]{1,0:T(1,128)S(1)}, f32[1,3072]{1,0:T(1,128)}, u32[]{:S(2)}) copy-start(f32[1,3072]{1,0:T(1,128)} %get-tuple-element.29) | copy-start | bytes 36868
  615.3 7.3 %copy-start.1 = (bf16[3078,2,128]{2,1,0:T(2,128)(2,1)S(1)}, bf16[3078,2,128]{2,1,0:T(2,128)(2,1)}, u32[]{:S(2)}) copy-start(bf16[3078,2,128]{2,1,0:T(2,128)(2,1)} %get-tuple-element.16) | copy-start | bytes 4727812
  621.4 2.4 copy-start

commit v5 on v4

--- a/solution.py
+++ b/solution.py
@@ -90,11 +90,11 @@
     def h_part(s, p, half):
         return H.at[s, rows_of(p), pl.ds(half * DH, DH)]
 
-    def d_g(s, par, e, half):
-        return rc(h_part(s, pX, half), h_part(s, pX, half), s_gs.at[par, e, half], s_gr.at[par, e, half], to_near[e])
-
-    def d_r(s, par, e):
-        return rc(h_part(s, pN[e], e), h_part(s, pN[e], e), s_rs.at[par, e], s_rr.at[par, e], to_near[1 - e])
+    def d_g(s, e, half):
+        return rc(h_part(s, pX, half), h_part(s, pX, half), s_gs.at[s, e, half], s_gr.at[s, e, half], to_near[e])
+
+    def d_r(s, e):
+        return rc(h_part(s, pN[e], e), h_part(s, pN[e], e), s_rs.at[s, e], s_rr.at[s, e], to_near[1 - e])
 
     def d_d(s, p):
         return rc(H.at[s, rows_of(p)], H.at[s, rows_of(p)], s_ds.at[s], s_dr.at[s], to_partner)
@@ -124,7 +124,7 @@
     def piece(l, k, wide, r):
         par = lax.rem(l, 2)
         if wide:
-            return WQF.at[par, pl.ds(pl.multiple_of(r * DQ, DQ), DQ), pl.ds(pl.multiple_of(k * hd, hd), hd)]
+            return WQF.at[par, k, pl.ds(pl.multiple_of(r * DQ, DQ), DQ), :]
         return WOF.at[par, pl.ds(pl.multiple_of(r * OQ + (k - (G + 2)) * OC, OC), OC), :]
 
     def fetched(k, wide):
@@ -173,17 +173,6 @@
 
     for w in prompt_copies(0) + small + [d_fetch(1, k, True) for k in range(3)] + wa_copies(0):
         w.start()
-    KV[...] = jnp.zeros(KV.shape, BF16)
-    for s in range(STREAMS):
-        H[s, TS:TS + DEC, :] = jnp.zeros((DEC, D), BF16)
-
-    def zero_kvr(l, _):
-        for pr in BOTH:
-            for kv in BOTH:
-                KVR[l, pr, kv, T:T + PAD, :] = jnp.zeros((PAD, hd), BF16)
-        return 0
-
-    lax.fori_loop(0, L, zero_kvr, 0)
 
     def normed(xf, gain):
         ms = jnp.mean(xf * xf, axis=-1, keepdims=True)
@@ -223,9 +212,63 @@
         live_2, _, fag_2 = state(m2)
         live_3, _, fag_3 = state(m3)
         live_c, frs_c, _ = state(mc)
-        heavy = jnp.logical_and(n >= 1, n < STREAMS)
+        heavy = jnp.logical_and(n >= 0, n < STREAMS)
         par_n, par_1 = lax.rem(n + 8, 2), lax.rem(m1 + 8, 2)
         s_n, s_1, s_2, s_3 = (lax.rem(m + 8, STREAMS) for m in (n, m1, m2, m3))
+
+        def pieces(t, fn, first=0):
+            r = lax.rem(t + 8, 8)
+
+            @when(t == first)
+            def _():
+                for k in range(3):
+                    fn(1, k, True)
+
+            @when(t >= 0, r == 0, lax.div(t, 8) + 1 < L)
+            def _():
+                for k in (3, 4):
+                    fn(lax.div(t, 8) + 1, k, True)
+
+            @when(t >= 0, r >= 1, r <= 3, lax.div(t, 8) + 1 < L)
+            def _():
+                fn(lax.div(t, 8) + 1, 4 + r, False)
+
+            @when(t >= 0, r >= 5, lax.div(t, 8) + 2 < L)
+            def _():
+                fn(lax.div(t, 8) + 2, r - 5, True)
+
+        def by_parity(k, even, odd):
+            if isinstance(k, int):
+                (odd if k % 2 else even)()
+            else:
+                when(lax.rem(k, 2) == 0)(even)
+                when(lax.rem(k, 2) == 1)(odd)
+
+        def arrived(l, k, wide):
+            opposite = lax.rem(j + 2, n_ho)
+            d_on(l, k, wide, opposite, {'ho': up}).wait_recv()
+            d_on(l, k, wide, opposite, {'ho': up}).wait_send()
+
+        def pass_on(l, k, wide):
+            d_up(l, k, wide, j).wait_recv()
+            d_down(l, k, wide, j).wait_recv()
+            by_parity(k, lambda: d_on(l, k, wide, down, {'ho': up}).start(),
+                      lambda: d_on(l, k, wide, up, {'ho': down}).start())
+            d_up(l, k, wide, j).wait_send()
+            d_down(l, k, wide, j).wait_send()
+
+        def spread(l, k, wide):
+            d_x(l, k, wide).wait_recv()
+            d_up(l, k, wide, j).start()
+            d_down(l, k, wide, j).start()
+            d_x(l, k, wide).wait_send()
+
+        def send_over(l, k, wide):
+            d_fetch(l, k, wide).wait()
+            d_x(l, k, wide).start()
+
+        pieces(n, send_over, -1)
+        pieces(n + 1, lambda l, k, wide: d_fetch(l, k, wide).start(), -1)
 
         def add(h, p):
             PB[par_n, h, p, c] = PB[par_n, h, p, c] + PR[par_n, h, p]
@@ -272,64 +315,6 @@
             d_c(par_n, s_n, 0).start()
             for h in BOTH:
                 add(h, pX)
-
-        def pieces(t, fn):
-            r = lax.rem(t + 8, 8)
-
-            @when(t == -1)
-            def _():
-                for k in range(3):
-                    fn(1, k, True)
-
-            @when(t >= 0, r == 0, lax.div(t, 8) + 1 < L)
-            def _():
-                for k in (3, 4):
-                    fn(lax.div(t, 8) + 1, k, True)
-
-            @when(t >= 0, r >= 1, r <= 3, lax.div(t, 8) + 1 < L)
-            def _():
-                fn(lax.div(t, 8) + 1, 4 + r, False)
-
-            @when(t >= 0, r >= 5, lax.div(t, 8) + 2 < L)
-            def _():
-                fn(lax.div(t, 8) + 2, r - 5, True)
-
-        def by_parity(k, even, odd):
-            if isinstance(k, int):
-                (odd if k % 2 else even)()
-            else:
-                when(lax.rem(k, 2) == 0)(even)
-                when(lax.rem(k, 2) == 1)(odd)
-
-        def arrived(l, k, wide):
-            opposite = lax.rem(j + 2, n_ho)
-            d_on(l, k, wide, opposite, {'ho': up}).wait_recv()
-            d_on(l, k, wide, opposite, {'ho': up}).wait_send()
-
-        def pass_on(l, k, wide):
-            d_up(l, k, wide, j).wait_recv()
-            d_down(l, k, wide, j).wait_recv()
-            by_parity(k, lambda: d_on(l, k, wide, down, {'ho': up}).start(),
-                      lambda: d_on(l, k, wide, up, {'ho': down}).start())
-            d_up(l, k, wide, j).wait_send()
-            d_down(l, k, wide, j).wait_send()
-
-        def spread(l, k, wide):
-            d_x(l, k, wide).wait_recv()
-            d_up(l, k, wide, j).start()
-            d_down(l, k, wide, j).start()
-            d_x(l, k, wide).wait_send()
-
-        def send_over(l, k, wide):
-            d_fetch(l, k, wide).wait()
-            d_x(l, k, wide).start()
-
-        pieces(n, send_over)
-
-        @when(n >= 0)
-        def _():
-            for e in BOTH:
-                pl.semaphore_wait(s_sync.at[e], 1)
 
         @when(live_1)
         def _():
@@ -364,17 +349,17 @@
                 hn = x_new[h] * inv * gain
                 H[s_1, rows_of(pX), cols] = jnp.where(last, x_new[h], hn).astype(BF16)
 
-            d_g(s_1, par_1, 0, 0).start()
+            d_g(s_1, 0, 0).start()
 
             @when(fag_1)
             def _():
-                d_g(s_1, par_1, 1, 1).start()
-
-            d_g(s_1, par_1, 0, 1).start()
+                d_g(s_1, 1, 1).start()
+
+            d_g(s_1, 0, 1).start()
 
             @when(fag_1)
             def _():
-                d_g(s_1, par_1, 1, 0).start()
+                d_g(s_1, 1, 0).start()
 
             d_d(s_1, pX).start()
 
@@ -397,32 +382,6 @@
                 for h in BOTH:
                     d_pr_home(par_1, h).wait_send()
 
-        @when(live_2)
-        def _():
-            par = lax.rem(m2, 2)
-            d_g(s_2, par, 0, 1).wait_recv()
-
-            @when(jnp.logical_not(fag_2))
-            def _():
-                d_g(s_2, par, 0, 0).wait_recv()
-
-            d_d(s_2, pQ).start()
-
-            @when(fag_2)
-            def _():
-                d_g(s_2, par, 1, 0).wait_recv()
-                d_d(s_2, pV).start()
-                for e in BOTH:
-                    d_r(s_2, par, e).wait_recv()
-                d_d(s_2, pO).start()
-                for half in BOTH:
-                    d_g(s_2, par, 1, half).wait_send()
-                for e in BOTH:
-                    d_r(s_2, par, e).wait_send()
-
-            for half in BOTH:
-                d_g(s_2, par, 0, half).wait_send()
-
         for full, blocks in ((True, CHIPS), (False, CHIPS // 2)):
             @when(live_3, fag_3 if full else jnp.logical_not(fag_3))
             def _():
@@ -437,6 +396,16 @@
 
         pieces(n - 4, arrived)
         pieces(n - 1, spread)
+
+        @when(n == 0)
+        def _():
+            def zero(l, _):
+                for pr in BOTH:
+                    for kv in BOTH:
+                        KVR[l, pr, kv, T:T + PAD, :] = jnp.zeros((PAD, hd), BF16)
+                return 0
+
+            lax.fori_loop(0, L, zero, 0)
 
         r8 = lax.rem(mc, 8)
         rows8 = lax.broadcasted_iota(jnp.int32, (8, hd), 0)
@@ -462,10 +431,10 @@
 
         @when(jnp.logical_or(r8 == 6, jnp.logical_and(r8 == 1, mc > 8)))
         def _():
-            d_e(2).wait_recv()
-            d_e(2).wait_send()
-            EX[E_C] = EX[E_B] + EX[E_IN2]
-            d_e(3).start()
+            d_e(1).wait_recv()
+            d_e(1).wait_send()
+            EX[E_B] = EX[E_A] + EX[E_IN1]
+            d_e(2).start()
 
         @when(jnp.logical_or(r8 == 7, jnp.logical_and(r8 == 2, mc > 8)))
         def _():
@@ -546,9 +515,10 @@
                 lpar = lax.rem(lq_c, 2)
 
                 def go(c0, c1):
-                    for f, w in enumerate((WQ, WQF.at[lpar])):
+                    other = jnp.concatenate([WQF[lpar, i] for i in range(c0 // hd, c1 // hd)], axis=1)
+                    for f, w in enumerate((WQ[:, c0:c1], other)):
                         QS[f * HS:(f + 1) * HS, c0:c1] = jnp.dot(
-                            H[sc, home, :], w[:, c0:c1], preferred_element_type=F32).astype(BF16)
+                            H[sc, home, :], w, preferred_element_type=F32).astype(BF16)
 
                 qkv_tiles(go)
 
@@ -574,25 +544,27 @@
                 d_kv(lq_c, 0, hp, sc, {'ho': up}).start()
                 d_kv(lq_c, 1, hp, sc, {'ho': up, 'tp': V * CORES + c}).start()
 
-            RT = tile_of(HS, 128)
-
-            def attn_tile(i, _):
-                g = lax.div(i, TS // RT)
-                r = lax.rem(i, TS // RT)
-                f = lax.div(r, HS // RT)
-                rows = pl.ds(pl.multiple_of(r * RT, RT), RT)
-                cols = pl.ds(pl.multiple_of(g * hd, hd), hd)
-                q = QS[rows, cols]
-                scores = lax.dot_general(q, KV[f, 0], (((1,), (1,)), ((), ())), preferred_element_type=F32) * scale
-                qpos = sc * HS + lax.rem(r, HS // RT) * RT + lax.broadcasted_iota(jnp.int32, (RT, T), 0)
-                kpos = lax.broadcasted_iota(jnp.int32, (RT, T), 1)
-                scores = jnp.where(qpos >= kpos, scores, -1e30)
-                e = jnp.exp(scores - jnp.max(scores, axis=-1, keepdims=True))
-                p = (e / jnp.sum(e, axis=-1, keepdims=True)).astype(BF16)
-                OS[rows, cols] = jnp.dot(p, KV[f, 1], preferred_element_type=F32).astype(BF16)
-                return 0
-
-            lax.fori_loop(0, G * (TS // RT), attn_tile, 0)
+            for s in range(STREAMS):
+                @when(sc == s)
+                def _():
+                    keys = (s + 1) * HS
+
+                    def attn_tile(i, _):
+                        g = lax.div(i, CORES)
+                        f = lax.rem(i, CORES)
+                        rows = pl.ds(pl.multiple_of(f * HS, HS), HS)
+                        cols = pl.ds(pl.multiple_of(g * hd, hd), hd)
+                        scores = lax.dot_general(QS[rows, cols], KV[f, 0, 0:keys, :], (((1,), (1,)), ((), ())),
+                                                 preferred_element_type=F32) * scale
+                        qpos = s * HS + lax.broadcasted_iota(jnp.int32, (HS, keys), 0)
+                        kpos = lax.broadcasted_iota(jnp.int32, (HS, keys), 1)
+                        scores = jnp.where(qpos >= kpos, scores, -1e30)
+                        e = jnp.exp(scores - jnp.max(scores, axis=-1, keepdims=True))
+                        p = (e / jnp.sum(e, axis=-1, keepdims=True)).astype(BF16)
+                        OS[rows, cols] = jnp.dot(p, KV[f, 1, 0:keys, :], preferred_element_type=F32).astype(BF16)
+                        return 0
+
+                    lax.fori_loop(0, CORES * G, attn_tile, 0)
 
         UT = tile_of(F, 256)
 
@@ -627,6 +599,31 @@
                 PB[par_n, e, pV, c] = PB[par_n, e, pV, c] + AR[par_n, e]
             d_c(par_n, s_n, 1).start()
             d_b(par_n, s_n, 1).start()
+
+        @when(live_2)
+        def _():
+            d_g(s_2, 0, 1).wait_recv()
+
+            @when(jnp.logical_not(fag_2))
+            def _():
+                d_g(s_2, 0, 0).wait_recv()
+
+            d_d(s_2, pQ).start()
+
+            @when(fag_2)
+            def _():
+                d_g(s_2, 1, 0).wait_recv()
+                d_d(s_2, pV).start()
+                for e in BOTH:
+                    d_r(s_2, e).wait_recv()
+                d_d(s_2, pO).start()
+                for half in BOTH:
+                    d_g(s_2, 1, half).wait_send()
+                for e in BOTH:
+                    d_r(s_2, e).wait_send()
+
+            for half in BOTH:
+                d_g(s_2, 0, half).wait_send()
 
         NT = tile_of(DH, 512)
 
@@ -679,15 +676,15 @@
         @when(live_1, fag_1)
         def _():
             for e in BOTH:
-                d_g(s_1, par_1, e, e).wait_recv()
-                d_r(s_1, par_1, e).start()
-
-        @when(jnp.logical_or(r8 == 5, jnp.logical_and(r8 == 0, mc > 0)))
-        def _():
-            d_e(1).wait_recv()
-            d_e(1).wait_send()
-            EX[E_B] = EX[E_A] + EX[E_IN1]
-            d_e(2).start()
+                d_g(s_1, e, e).wait_recv()
+                d_r(s_1, e).start()
+
+        @when(jnp.logical_or(r8 == 6, jnp.logical_and(r8 == 1, mc > 8)))
+        def _():
+            d_e(2).wait_recv()
+            d_e(2).wait_send()
+            EX[E_C] = EX[E_B] + EX[E_IN2]
+            d_e(3).start()
 
         @when(live_c, r8 == 4)
         def _():
@@ -748,12 +745,8 @@
 
         @when(n >= 0)
         def _():
-            pieces(n + 1, lambda l, k, wide: d_fetch(l, k, wide).start())
-
-        @when(n == -1)
-        def _():
-            for k in (3, 4):
-                d_fetch(1, k, True).start()
+            for e in BOTH:
+                pl.semaphore_wait(s_sync.at[e], 1)
 
         return 0
 
@@ -819,7 +812,7 @@
                 pltpu.VMEM((L, 2, 2, T + PAD, hd), BF16),
                 pltpu.VMEM((D, (G + 2) * hd), BF16),
                 pltpu.VMEM((G * hd, D), BF16),
-                pltpu.VMEM((2, D, (G + 2) * hd), BF16),
+                pltpu.VMEM((2, G + 2, D, hd), BF16),
                 pltpu.VMEM((2, G * hd, D), BF16),
                 pltpu.VMEM((G + 2, D // n_ho, hd), BF16),
                 pltpu.VMEM((3, G * hd // n_ho // 3, D), BF16),
@@ -836,7 +829,7 @@
                 pltpu.VMEM((2, T + 8, 2, hd), BF16),
                 *map(dma, (two, two, two, two)),
                 *map(dma, (by_stream, by_stream, by_stream, by_stream)),
-                *map(dma, (two + two[:1], two + two[:1], two, two)),
+                *map(dma, (by_stream + two[:1], by_stream + two[:1], by_stream, by_stream)),
                 *map(dma, (four, four)),
                 *map(dma, (two[:1], (L,) + two[:1])),
                 *map(dma, ((G + 3,), eight, (3,))),

time: 626 us -> 618 us (0.987)
  Pallas kernels: 615 us -> 607 us
    pallas_call x1, Pallas kernels: 615 us -> 607 us  [per_device(): pl.pallas_call(functools.partial(body, (n_ho, n_tp, L, T, D, G, hd, F)),...]
where the time goes in v5:
time: 618 us
  Pallas kernels  607 us (98%)
  local copies, waits for them, and re-layouts  9.6 us (2%)
    pallas_call x1, Pallas kernels, per_device(): pl.pallas_call(functools.partial(body, (n_ho, n_tp, L, T, D, G, hd, F)),...  607 us

profile of v5, /device:TPU:97, one launch (start us, length us, event | category | flops | bytes accessed | tf_op | source)
XLA Modules:
  0.0 617.7 jit_solution(18262127056403387467)
XLA Ops:
  0.6 607.4 %serve.1 = (bf16[528,3072]{1,0:T(8,128)(2,1)}, bf16[528,3072]{1,0:T(8,128)(2,1)}, f32[1,3072]{1,0:T(1,128)}, f32[1,3072]{1,0:T(1,128)}, bf16[3078,2,128]{2,1,0:T(2,128)(2,1)}, /*index=5*/bf16[3078,2,128]{2,1,0:T(2,128)(2,1)}) custom-call(bf16[4,512,3072]{2,1,0:T(8,128)(2,1)} %pa.1, bf16[4,512,3072]{2,1,0:T(8,128)(2,1)} %pb.1, bf16[1,3072]{1,0:T(2,128)(2,1)} %fa.1, ...), custom_call_target="tpu_custom_call" | custom-call | flops 154618822656 | bytes 301989888 | tf_op jit(solution)/shard_map/serve/pallas_call | solution.py:792
  608.0 0.0 copy-start.3
  608.0 0.0 copy-start.2
  608.0 0.0 copy-start.1
  608.1 6.1 slice_bitcast_fusion
  614.2 0.0 copy-start
  614.2 0.0 copy-done.3
  614.2 0.6 copy.21
  614.8 0.0 copy-done.2
  614.8 0.6 copy.22
  615.4 0.0 copy-done.1
  615.4 1.1 copy.23
  616.5 0.0 copy-done
  616.5 1.1 copy.24
Async XLA Ops:
  608.0 6.1 copy-start.3
  608.0 6.7 %copy-start.2 = (f32[1,3072]{1,0:T(1,128)S(1)}, f32[1,3072]{1,0:T(1,128)}, u32[]{:S(2)}) copy-start(f32[1,3072]{1,0:T(1,128)} %get-tuple-element.29) | copy-start | bytes 36868
  608.0 7.3 %copy-start.1 = (bf16[3078,2,128]{2,1,0:T(2,128)(2,1)S(1)}, bf16[3078,2,128]{2,1,0:T(2,128)(2,1)}, u32[]{:S(2)}) copy-start(bf16[3078,2,128]{2,1,0:T(2,128)(2,1)} %get-tuple-element.16) | copy-start | bytes 4727812
  614.2 2.4 copy-start

commit v6 on v5

--- a/solution.py
+++ b/solution.py
@@ -422,22 +422,25 @@
                     EX[slot_, t] = acc
             d_e(0).start()
 
-        @when(jnp.logical_or(r8 == 5, jnp.logical_and(r8 == 0, mc > 0)))
-        def _():
+        def sum_cores():
             d_e(0).wait_recv()
             d_e(0).wait_send()
             EX[E_A] = EX[E_A] + EX[E_IN0]
             d_e(1).start()
 
-        @when(jnp.logical_or(r8 == 6, jnp.logical_and(r8 == 1, mc > 8)))
-        def _():
+        def sum_pair():
             d_e(1).wait_recv()
             d_e(1).wait_send()
             EX[E_B] = EX[E_A] + EX[E_IN1]
             d_e(2).start()
 
-        @when(jnp.logical_or(r8 == 7, jnp.logical_and(r8 == 2, mc > 8)))
-        def _():
+        def sum_all():
+            d_e(2).wait_recv()
+            d_e(2).wait_send()
+            EX[E_C] = EX[E_B] + EX[E_IN2]
+            d_e(3).start()
+
+        def decode_update():
             d_e(3).wait_recv()
             d_e(3).wait_send()
             for slot_, half in ((E_C, c), (E_IN3, 1 - c)):
@@ -453,9 +456,12 @@
             def _():
                 decode_norm(g2[pl.ds(lq, 1), :])
 
-            @when(r8 == 2, mc < NS)
+            @when(r8 == 3, mc < NS)
             def _():
                 decode_norm(g1[pl.ds(jnp.minimum(lq, L - 1), 1), :])
+
+        when(r8 == 0, mc > 0)(sum_cores)
+        when(jnp.logical_or(r8 == 7, jnp.logical_and(r8 == 3, mc > 8)))(decode_update)
 
         par_c = lax.rem(mc, 2)
         sc = lax.rem(mc, STREAMS)
@@ -491,7 +497,7 @@
         def _():
             @when(sc == 0)
             def _():
-                for w in wa_copies(lq_c):
+                for w in wa_copies(lq_c)[:-1]:
                     w.wait()
 
                 @when(mc == 0)
@@ -566,7 +572,7 @@
 
                     lax.fori_loop(0, CORES * G, attn_tile, 0)
 
-        UT = tile_of(F, 256)
+        UT, NT = tile_of(F, 256), tile_of(DH, 512)
 
         @when(mlp_c)
         def _():
@@ -599,92 +605,6 @@
                 PB[par_n, e, pV, c] = PB[par_n, e, pV, c] + AR[par_n, e]
             d_c(par_n, s_n, 1).start()
             d_b(par_n, s_n, 1).start()
-
-        @when(live_2)
-        def _():
-            d_g(s_2, 0, 1).wait_recv()
-
-            @when(jnp.logical_not(fag_2))
-            def _():
-                d_g(s_2, 0, 0).wait_recv()
-
-            d_d(s_2, pQ).start()
-
-            @when(fag_2)
-            def _():
-                d_g(s_2, 1, 0).wait_recv()
-                d_d(s_2, pV).start()
-                for e in BOTH:
-                    d_r(s_2, e).wait_recv()
-                d_d(s_2, pO).start()
-                for half in BOTH:
-                    d_g(s_2, 1, half).wait_send()
-                for e in BOTH:
-                    d_r(s_2, e).wait_send()
-
-            for half in BOTH:
-                d_g(s_2, 0, half).wait_send()
-
-        NT = tile_of(DH, 512)
-
-        def at_cols(t):
-            return pl.ds(pl.multiple_of(t * NT, NT), NT)
-
-        @when(attn_c, mc < 8)
-        def _():
-            for h in BOTH:
-                def out_tile(t, _):
-                    cols = pl.ds(pl.multiple_of(h * DH + t * NT, NT), NT)
-                    val = jnp.dot(OS[...], WO[:, cols], preferred_element_type=F32)
-                    PB[par_c, h, :, :, :, at_cols(t)] = val.astype(BF16).reshape(CHIPS, CORES, BR, NT)
-                    return 0
-
-                lax.fori_loop(0, DH // NT, out_tile, 0)
-                d_pr(par_c, h).start()
-
-        @when(attn_c, mc >= 8)
-        def _():
-            for h in BOTH:
-                def out_tile(t, _):
-                    cols = pl.ds(pl.multiple_of(h * DH + t * NT, NT), NT)
-                    val = jnp.dot(OS[0:HS, :], WO[:, cols], preferred_element_type=F32)
-                    val = val + jnp.dot(OS[HS:TS, :], WOF[lax.rem(lq_c, 2), :, cols], preferred_element_type=F32)
-                    PB[par_c, h, pl.ds(hp * 2, 2), :, :, at_cols(t)] = val.astype(BF16).reshape(2, CORES, BR, NT)
-                    return 0
-
-                lax.fori_loop(0, DH // NT, out_tile, 0)
-                d_pr_home(par_c, h).start()
-
-        @when(mlp_c)
-        def _():
-            for h in BOTH:
-                def down_tile(t, _):
-                    cols = pl.ds(pl.multiple_of(h * DH + t * NT, NT), NT)
-                    val = jnp.dot(US[...], WD[:, cols], preferred_element_type=F32)
-                    PB[par_c, h, :, :, :, at_cols(t)] = val[0:TS].astype(BF16).reshape(CHIPS, CORES, BR, NT)
-                    DP[:, cols] = val[TS:TS + 8]
-                    return 0
-
-                lax.fori_loop(0, DH // NT, down_tile, 0)
-                d_pr(par_c, h).start()
-
-        @when(n < NS + 2)
-        def _():
-            for e in BOTH:
-                pl.semaphore_signal(s_sync.at[e], inc=1, device_id=to_near[e], device_id_type=MESH)
-
-        @when(live_1, fag_1)
-        def _():
-            for e in BOTH:
-                d_g(s_1, e, e).wait_recv()
-                d_r(s_1, e).start()
-
-        @when(jnp.logical_or(r8 == 6, jnp.logical_and(r8 == 1, mc > 8)))
-        def _():
-            d_e(2).wait_recv()
-            d_e(2).wait_send()
-            EX[E_C] = EX[E_B] + EX[E_IN2]
-            d_e(3).start()
 
         @when(live_c, r8 == 4)
         def _():
@@ -731,6 +651,95 @@
             def _():
                 for w in wa_copies(lax.div(mc, 8) + 1):
                     w.start()
+
+        when(r8 == 1, mc > 8)(sum_pair)
+        when(r8 == 2, mc > 8)(sum_all)
+
+        @when(live_2)
+        def _():
+            d_g(s_2, 0, 1).wait_recv()
+
+            @when(jnp.logical_not(fag_2))
+            def _():
+                d_g(s_2, 0, 0).wait_recv()
+
+            d_d(s_2, pQ).start()
+
+            @when(fag_2)
+            def _():
+                d_g(s_2, 1, 0).wait_recv()
+                d_d(s_2, pV).start()
+                for e in BOTH:
+                    d_r(s_2, e).wait_recv()
+                d_d(s_2, pO).start()
+                for half in BOTH:
+                    d_g(s_2, 1, half).wait_send()
+                for e in BOTH:
+                    d_r(s_2, e).wait_send()
+
+            for half in BOTH:
+                d_g(s_2, 0, half).wait_send()
+
+
+        def at_cols(t):
+            return pl.ds(pl.multiple_of(t * NT, NT), NT)
+
+        @when(attn_c, sc == 0)
+        def _():
+            wa_copies(lq_c)[-1].wait()
+
+        @when(attn_c, mc < 8)
+        def _():
+            for h in BOTH:
+                def out_tile(t, _):
+                    cols = pl.ds(pl.multiple_of(h * DH + t * NT, NT), NT)
+                    val = jnp.dot(OS[...], WO[:, cols], preferred_element_type=F32)
+                    PB[par_c, h, :, :, :, at_cols(t)] = val.astype(BF16).reshape(CHIPS, CORES, BR, NT)
+                    return 0
+
+                lax.fori_loop(0, DH // NT, out_tile, 0)
+                d_pr(par_c, h).start()
+
+        @when(attn_c, mc >= 8)
+        def _():
+            for h in BOTH:
+                def out_tile(t, _):
+                    cols = pl.ds(pl.multiple_of(h * DH + t * NT, NT), NT)
+                    val = jnp.dot(OS[0:HS, :], WO[:, cols], preferred_element_type=F32)
+                    val = val + jnp.dot(OS[HS:TS, :], WOF[lax.rem(lq_c, 2), :, cols], preferred_element_type=F32)
+                    PB[par_c, h, pl.ds(hp * 2, 2), :, :, at_cols(t)] = val.astype(BF16).reshape(2, CORES, BR, NT)
+                    return 0
+
+                lax.fori_loop(0, DH // NT, out_tile, 0)
+                d_pr_home(par_c, h).start()
+
+        @when(mlp_c)
+        def _():
+            for h in BOTH:
+                def down_tile(t, _):
+                    cols = pl.ds(pl.multiple_of(h * DH + t * NT, NT), NT)
+                    val = jnp.dot(US[...], WD[:, cols], preferred_element_type=F32)
+                    PB[par_c, h, :, :, :, at_cols(t)] = val[0:TS].astype(BF16).reshape(CHIPS, CORES, BR, NT)
+                    DP[:, cols] = val[TS:TS + 8]
+                    return 0
+
+                lax.fori_loop(0, DH // NT, down_tile, 0)
+                d_pr(par_c, h).start()
+
+        @when(n < NS + 2)
+        def _():
+            for e in BOTH:
+                pl.semaphore_signal(s_sync.at[e], inc=1, device_id=to_near[e], device_id_type=MESH)
+
+        @when(live_1, fag_1)
+        def _():
+            for e in BOTH:
+                d_g(s_1, e, e).wait_recv()
+                d_r(s_1, e).start()
+
+        when(r8 == 4)(sum_cores)
+        when(r8 == 5)(sum_pair)
+        when(r8 == 6)(sum_all)
 
         @when(live_c, r8 == 7)
         def _():

time: 618 us -> 612 us (level)
  no operation moved by 1% of the time
where the time goes in v6:
time: 612 us
  Pallas kernels  602 us (98%)
  local copies, waits for them, and re-layouts  9.6 us (2%)
    pallas_call x1, Pallas kernels, per_device(): pl.pallas_call(functools.partial(body, (n_ho, n_tp, L, T, D, G, hd, F)),...  602 us

profile of v6, /device:TPU:97, one launch (start us, length us, event | category | flops | bytes accessed | tf_op | source)
XLA Modules:
  0.0 612.3 jit_solution(12772742696252305085)
XLA Ops:
  0.6 602.0 %serve.1 = (bf16[528,3072]{1,0:T(8,128)(2,1)}, bf16[528,3072]{1,0:T(8,128)(2,1)}, f32[1,3072]{1,0:T(1,128)}, f32[1,3072]{1,0:T(1,128)}, bf16[3078,2,128]{2,1,0:T(2,128)(2,1)}, /*index=5*/bf16[3078,2,128]{2,1,0:T(2,128)(2,1)}) custom-call(bf16[4,512,3072]{2,1,0:T(8,128)(2,1)} %pa.1, bf16[4,512,3072]{2,1,0:T(8,128)(2,1)} %pb.1, bf16[1,3072]{1,0:T(2,128)(2,1)} %fa.1, ...), custom_call_target="tpu_custom_call" | custom-call | flops 154618822656 | bytes 301989888 | tf_op jit(solution)/shard_map/serve/pallas_call | solution.py:801
  602.7 0.0 copy-start.3
  602.7 0.0 copy-start.2
  602.7 0.0 copy-start.1
  602.7 6.1 slice_bitcast_fusion
  608.8 0.0 copy-start
  608.8 0.0 copy-done.3
  608.8 0.6 copy.21
  609.4 0.0 copy-done.2
  609.4 0.6 copy.22
  610.0 0.0 copy-done.1
  610.0 1.1 copy.23
  611.2 0.0 copy-done
  611.2 1.1 copy.24
Async XLA Ops:
  602.7 6.1 %copy-start.3 = (f32[1,3072]{1,0:T(1,128)S(1)}, f32[1,3072]{1,0:T(1,128)}, u32[]{:S(2)}) copy-start(f32[1,3072]{1,0:T(1,128)} %get-tuple-element.28) | copy-start | bytes 36868
  602.7 6.7 %copy-start.2 = (f32[1,3072]{1,0:T(1,128)S(1)}, f32[1,3072]{1,0:T(1,128)}, u32[]{:S(2)}) copy-start(f32[1,3072]{1,0:T(1,128)} %get-tuple-element.29) | copy-start | bytes 36868
  602.7 7.3 %copy-start.1 = (bf16[3078,2,128]{2,1,0:T(2,128)(2,1)S(1)}, bf16[3078,2,128]{2,1,0:T(2,128)(2,1)}, u32[]{:S(2)}) copy-start(bf16[3078,2,128]{2,1,0:T(2,128)(2,1)} %get-tuple-element.16) | copy-start | bytes 4727812
  608.8 2.4 copy-start

commit v7 on v6

--- a/solution.py
+++ b/solution.py
@@ -572,7 +572,8 @@
 
                     lax.fori_loop(0, CORES * G, attn_tile, 0)
 
-        UT, NT = tile_of(F, 256), tile_of(DH, 512)
+        rows_of_mlp = ((TS, sc < STREAMS - 1), (TS + DEC, sc == STREAMS - 1))
+        UT, NT = tile_of(F, 512), tile_of(DH, 512)
 
         @when(mlp_c)
         def _():
@@ -581,14 +582,17 @@
                 for w in wm_copies(lq_c):
                     w.wait()
 
-            def gate_up(i, _):
-                cols = pl.ds(pl.multiple_of(i * UT, UT), UT)
-                gate = jnp.dot(H[sc], WG[:, cols], preferred_element_type=F32)
-                up_ = jnp.dot(H[sc], WU[:, cols], preferred_element_type=F32)
-                US[:, cols] = (gate * (1.0 / (1.0 + jnp.exp(-gate))) * up_).astype(BF16)
-                return 0
-
-            lax.fori_loop(0, F // UT, gate_up, 0)
+            for rows, these in rows_of_mlp:
+                @when(these)
+                def _():
+                    def gate_up(i, _):
+                        cols = pl.ds(pl.multiple_of(i * UT, UT), UT)
+                        gate = jnp.dot(H[sc, 0:rows], WG[:, cols], preferred_element_type=F32)
+                        up_ = jnp.dot(H[sc, 0:rows], WU[:, cols], preferred_element_type=F32)
+                        US[0:rows, cols] = (gate * (1.0 / (1.0 + jnp.exp(-gate))) * up_).astype(BF16)
+                        return 0
+
+                    lax.fori_loop(0, F // UT, gate_up, 0)
 
         @when(live_n, frs_n, jnp.logical_not(heavy))
         def _():
@@ -713,18 +717,20 @@
                 lax.fori_loop(0, DH // NT, out_tile, 0)
                 d_pr_home(par_c, h).start()
 
-        @when(mlp_c)
-        def _():
-            for h in BOTH:
-                def down_tile(t, _):
-                    cols = pl.ds(pl.multiple_of(h * DH + t * NT, NT), NT)
-                    val = jnp.dot(US[...], WD[:, cols], preferred_element_type=F32)
-                    PB[par_c, h, :, :, :, at_cols(t)] = val[0:TS].astype(BF16).reshape(CHIPS, CORES, BR, NT)
-                    DP[:, cols] = val[TS:TS + 8]
-                    return 0
-
-                lax.fori_loop(0, DH // NT, down_tile, 0)
-                d_pr(par_c, h).start()
+        for rows, these in rows_of_mlp:
+            @when(mlp_c, these)
+            def _():
+                for h in BOTH:
+                    def down_tile(t, _):
+                        cols = pl.ds(pl.multiple_of(h * DH + t * NT, NT), NT)
+                        val = jnp.dot(US[0:rows, :], WD[:, cols], preferred_element_type=F32)
+                        PB[par_c, h, :, :, :, at_cols(t)] = val[0:TS].astype(BF16).reshape(CHIPS, CORES, BR, NT)
+                        if rows > TS:
+                            DP[:, cols] = val[TS:TS + 8]
+                        return 0
+
+                    lax.fori_loop(0, DH // NT, down_tile, 0)
+                    d_pr(par_c, h).start()
 
         @when(n < NS + 2)
         def _():

time: 612 us -> 612 us (level)
  no operation moved by 1% of the time
where the time goes in v7:
time: 612 us
  Pallas kernels  601 us (98%)
  local copies, waits for them, and re-layouts  9.6 us (2%)
    pallas_call x1, Pallas kernels, per_device(): pl.pallas_call(functools.partial(body, (n_ho, n_tp, L, T, D, G, hd, F)),...  601 us

profile of v7, /device:TPU:97, one launch (start us, length us, event | category | flops | bytes accessed | tf_op | source)
XLA Modules:
  0.0 611.6 jit_solution(10939646442773769012)
XLA Ops:
  0.6 601.3 %serve.1 = (bf16[528,3072]{1,0:T(8,128)(2,1)}, bf16[528,3072]{1,0:T(8,128)(2,1)}, f32[1,3072]{1,0:T(1,128)}, f32[1,3072]{1,0:T(1,128)}, bf16[3078,2,128]{2,1,0:T(2,128)(2,1)}, /*index=5*/bf16[3078,2,128]{2,1,0:T(2,128)(2,1)}) custom-call(bf16[4,512,3072]{2,1,0:T(8,128)(2,1)} %pa.1, bf16[4,512,3072]{2,1,0:T(8,128)(2,1)} %pb.1, bf16[1,3072]{1,0:T(2,128)(2,1)} %fa.1, ...), custom_call_target="tpu_custom_call" | custom-call | flops 154618822656 | bytes 301989888 | tf_op jit(solution)/shard_map/serve/pallas_call | solution.py:807
  601.9 0.0 copy-start.3
  602.0 0.0 copy-start.2
  602.0 0.0 copy-start.1
  602.0 6.1 slice_bitcast_fusion
  608.1 0.0 copy-start
  608.1 0.0 copy-done.3
  608.1 0.6 copy.21
  608.7 0.0 copy-done.2
  608.7 0.6 copy.22
  609.3 0.0 copy-done.1
  609.3 1.1 copy.23
  610.4 0.0 copy-done
  610.4 1.1 copy.24
Async XLA Ops:
  601.9 6.1 %copy-start.3 = (f32[1,3072]{1,0:T(1,128)S(1)}, f32[1,3072]{1,0:T(1,128)}, u32[]{:S(2)}) copy-start(f32[1,3072]{1,0:T(1,128)} %get-tuple-element.28) | copy-start | bytes 36868
  602.0 6.7 %copy-start.2 = (f32[1,3072]{1,0:T(1,128)S(1)}, f32[1,3072]{1,0:T(1,128)}, u32[]{:S(2)}) copy-start(f32[1,3072]{1,0:T(1,128)} %get-tuple-element.29) | copy-start | bytes 36868
  602.0 7.3 %copy-start.1 = (bf16[3078,2,128]{2,1,0:T(2,128)(2,1)S(1)}, bf16[3078,2,128]{2,1,0:T(2,128)(2,1)}, u32[]{:S(2)}) copy-start(bf16[3078,2,128]{2,1,0:T(2,128)(2,1)} %get-tuple-element.16) | copy-start | bytes 4727812
  608.1 2.4 copy-start
